TPU v7x, 32 devices: a 4x4x1 block of a 4x4x8 slice. The times are simulated.
32 devices in a mesh: dp: 1 (over z), tp: 32 (over y, x, core).
Axes of the slice: x: 4, y: 4, z: 1, core: 2. Of those that a mesh axis runs over, the one named last changes fastest.
The devices are a block of a 4x4x8 slice.
Arguments:
- hidden: bfloat16 [8192, 1024], P(('dp', 'tp'))
- w_two: bfloat16 [1024, 1024], replicated
- ln_scale: float32 [2, 1024], replicated
- ln_shift: float32 [2, 1024], replicated
- embed: bfloat16 [53248, 1024], P('tp')
- targets: int32 [2, 8192], P(None, ('dp', 'tp'))
- loss_mask: int32 [2, 8192], P(None, ('dp', 'tp'))
Outputs:
- output 1: float32 [2, 8192], P(None, ('dp', 'tp'))
- output 2: float32 [1], P('dp')
- output 3: bfloat16 [8192, 1024], P(('dp', 'tp'))
- output 4: float32 [53248, 1024], P(('dp', 'tp'))
- output 5: float32 [1024, 1024], P('dp')
- output 6: float32 [2, 1024], P('dp')
- output 7: float32 [2, 1024], P('dp')
All inputs are finite; a program needn't handle non-finite values.
Results may differ from a plain program's by a relative error of at most 0.00599148.
Values are sent between devices in bfloat16 or wider.
A program may use at most 768 MiB of HBM per device.

v0:
```python
import jax
import jax.numpy as jnp
from jax import lax
from jax.sharding import PartitionSpec as P

LN_EPS = 1e-5


def layer_norm(values, gain, bias):
    mean_val = jnp.mean(values, axis=-1, keepdims=True)
    centered = values - mean_val
    variance = jnp.mean(centered * centered, axis=-1, keepdims=True)
    return centered * lax.rsqrt(variance + LN_EPS) * gain + bias


def solution(mesh):
    tok_spec = P(('dp', 'tp'), None)
    row_spec = P(None, ('dp', 'tp'))

    def device_step(hidden, w_two, ln_scale, ln_shift, embed, targets, loss_mask):
        tok_rows = hidden.shape[0]
        shard_rows = embed.shape[0]
        shard_idx = lax.axis_index('tp')
        proj_out = jnp.dot(hidden, w_two, preferred_element_type=jnp.float32).astype(jnp.bfloat16)
        norm_input = jnp.stack([hidden.astype(jnp.float32), proj_out.astype(jnp.float32)])
        normed, ln_back = jax.vjp(jax.vmap(layer_norm), norm_input, ln_scale, ln_shift)
        x_loc = normed.astype(jnp.bfloat16)
        x_all = lax.all_gather(x_loc, 'tp', axis=1, tiled=True)
        int_all = lax.all_gather(jnp.stack([targets, loss_mask]), 'tp', axis=2, tiled=True)
        tgt_all = int_all[0]
        mask_all = int_all[1].astype(jnp.float32)
        logits = jnp.einsum('hsd,vd->hsv', x_all, embed, preferred_element_type=jnp.float32)
        local_max = jnp.max(logits, axis=-1)
        exp_loc = jnp.exp(logits - local_max[..., None])
        col_ids = lax.broadcasted_iota(jnp.int32, (1, 1, shard_rows), 2) + shard_idx * shard_rows
        is_target = col_ids == tgt_all[..., None]
        tgt_loc = jnp.sum(jnp.where(is_target, logits, 0.0), axis=-1)
        glob_max = lax.pmax(local_max, 'tp')
        part_stats = jnp.stack([jnp.sum(exp_loc, axis=-1) * jnp.exp(local_max - glob_max), tgt_loc])
        glob_stats = lax.psum(part_stats, 'tp')
        log_norm = glob_max + jnp.log(glob_stats[0])
        token_count = jnp.sum(mask_all, axis=1)
        weight = mask_all / token_count[:, None]
        loss_all = (log_norm - glob_stats[1]) * mask_all
        total_loss = jnp.sum(loss_all / token_count[:, None]).reshape(1)
        token_loss = lax.dynamic_slice_in_dim(loss_all, shard_idx * tok_rows, tok_rows, axis=1)
        softmax_val = exp_loc * jnp.exp(local_max - log_norm)[..., None]
        d_logits = (jnp.where(is_target, softmax_val - 1.0, softmax_val) * weight[..., None]).astype(jnp.bfloat16)
        d_embed = jnp.einsum('hsv,hsd->vd', d_logits, x_all, preferred_element_type=jnp.float32)
        dx_part = jnp.einsum('hsv,vd->hsd', d_logits, embed, preferred_element_type=jnp.float32)
        dx_loc = lax.psum_scatter(dx_part, 'tp', scatter_dimension=1, tiled=True)
        d_norm_in, d_scale_part, d_shift_part = ln_back(dx_loc)
        d_proj = d_norm_in[1].astype(jnp.bfloat16)
        d_hidden = (d_norm_in[0] + jnp.einsum('td,ed->te', d_proj, w_two, preferred_element_type=jnp.float32)).astype(jnp.bfloat16)
        d_w_part = jnp.einsum('te,td->ed', hidden, d_proj, preferred_element_type=jnp.float32)
        d_w_two, d_scale, d_shift = lax.psum((d_w_part, d_scale_part, d_shift_part), 'tp')
        return token_loss, total_loss, d_hidden, d_embed, d_w_two, d_scale, d_shift

    return jax.shard_map(device_step, mesh=mesh,
                         in_specs=(tok_spec, P(), P(), P(), P('tp', None), row_spec, row_spec),
                         out_specs=(row_spec, P('dp'), tok_spec, tok_spec, P('dp', None), P('dp', None), P('dp', None)),
                         check_vma=False)
```

profile of v0, /device:TPU:97, one launch (start us, length us, event | category | flops | bytes accessed | tf_op | source)
XLA Modules:
  0.0 922.5 jit_solution(2314949962943256519)
XLA Ops:
  7.2 0.0 copy-start
  7.2 0.0 copy-start.11
  7.2 0.1 all-gather.2.cloned.1.call-start
  7.3 0.0 copy-start.2
  7.3 2.6 fusion.20
  9.9 0.0 copy-start.5
  9.9 0.2 convert_reduce_fusion
  10.2 0.0 copy-start.20
  10.2 0.0 copy-start.21
  10.2 0.4 fusion.17
  10.6 0.6 copy-done.17
  11.2 0.0 copy-start.15
  11.2 0.6 copy-done.15
  11.8 1.4 fusion.15
  13.2 0.1 all-gather.2.cloned.1.call-update
  13.3 0.1 all-reduce.5.cloned.1.call-start
  13.4 33.4 %all_gather.7 = s32[2,2,8192]{2,1,0:T(2,128)S(1)} all-gather(s32[2,2,256]{2,1,0:T(2,128)S(1)} %pad_add_fusion), channel_id=1, replica_groups=mesh['dp'=1,'tp'=32] {'tp'}, dimensions={2}, use_global_device_ids=true | all-gather | bytes 135168 | tf_op jit(solution)/shard_map/all_gather | solution.py:29
  46.8 0.0 copy-start.10
  46.8 0.6 copy-done.10
  47.5 79.0 %all-gather.2.cloned.1.call-done = bf16[2,8192,1024]{2,1,0:T(8,128)(2,1)} async-done(((bf16[2,256,1024]{2,1,0:T(8,128)(2,1)}), bf16[2,8192,1024]{2,1,0:T(8,128)(2,1)}) %all-gather.2.cloned.1.call-update) | async-done | bytes 33554448 | tf_op jit(solution)/shard_map/all_gather | solution.py:28
  126.5 66.2 %fusion.33 = (f32[2,8192]{1,0:T(2,128)}, f32[2,8192,1664]{1,2,0:T(8,128)}) fusion(bf16[2,8192,1024]{2,1,0:T(8,128)(2,1)} %all-gather.2.cloned.1.call-done, bf16[1664,1024]{1,0:T(8,128)(2,1)S(1)} %copy-done), kind=kOutput, calls=%fused_computation.60 | convolution fusion | flops 55861821440 | bytes 146079744 | tf_op jit(solution)/shard_map/hsd,vd->hsv/dot_general | solution.py:32
  192.7 0.1 all-reduce.5.cloned.1.call-update
  192.7 0.1 all-reduce.7.cloned.1.call-start
  192.8 37.6 %fusion.3 = (f32[2,8192]{1,0:T(2,128)}, f32[2,8192]{1,0:T(2,128)}) fusion(f32[2,8192,1664]{1,2,0:T(8,128)} %get-tuple-element.27, f32[2,8192]{1,0:T(2,128)} %get-tuple-element.26, s32[2,8192]{1,0:T(2,128)S(1)} %slice_bitcast_fusion.2, s32[1664]{0:T(1024)S(1)} %iota_add_fusion), kind=kLoop, calls=%fused_computation.6 | loop fusion | flops 136282112 | bytes 109320704 | tf_op jit(solution)/shard_map/reduce_sum | solution.py:39
  230.4 52.5 %all-reduce.5.cloned.1.call-done = f32[2,8192]{1,0:T(2,128)} async-done(((f32[2,8192]{1,0:T(2,128)}), f32[2,8192]{1,0:T(2,128)}) %all-reduce.5.cloned.1.call-update) | async-done | bytes 65552 | tf_op jit(solution)/shard_map/pmax | solution.py:38
  282.8 0.9 multiply_bitcast_fusion
  283.8 1.6 pad_maximum_fusion.1
  285.3 0.1 all-reduce.7.cloned.1.call-update
  285.4 0.2 reduce-scatter.2.cloned.1.call-start
  285.7 1.0 fusion.29
  286.7 92.2 %all-reduce.7.cloned.1.call-done = f32[2,2,8192]{2,1,0:T(2,128)} async-done(((f32[2,2,8192]{2,1,0:T(2,128)}), f32[2,2,8192]{2,1,0:T(2,128)}) %all-reduce.7.cloned.1.call-update) | async-done | bytes 131088 | tf_op jit(solution)/shard_map/psum | solution.py:40
  378.9 2.3 divide_reduce_fusion
  381.2 53.1 %fusion.2 = bf16[2,8192,1664]{1,2,0:T(8,128)(2,1)} fusion(f32[2,8192,1664]{1,2,0:T(8,128)} %get-tuple-element.27, f32[2,8192]{1,0:T(2,128)S(1)} %get-tuple-element.25, f32[2,8192]{1,0:T(2,128)S(1)} %get-tuple-element.24, s32[2,8192]{1,0:T(2,128)S(1)} %slice_bitcast_fusion.2, f32[2,8192]{1,0:T(2,128)S(1)} %copy-done.9, s32[1664]{0:T(1024)S(1)} %iota_add_fusion), kind=kLoop, calls=%fused_computation.4 | loop fusion | flops 190840832 | bytes 163846656 | tf_op jit(solution)/shard_map/convert_element_type | solution.py:48
  434.3 69.2 %fusion.4 = f32[2,8192,1024]{2,1,0:T(8,128)} fusion(bf16[2,8192,1664]{1,2,0:T(8,128)(2,1)} %fusion.2, bf16[1664,1024]{1,0:T(8,128)(2,1)S(1)} %copy-done), kind=kOutput, calls=%fused_computation.8 | convolution fusion | flops 55834574848 | bytes 125042688 | tf_op jit(solution)/shard_map/hsv,vd->hsd/dot_general | solution.py:50
  503.5 0.1 reduce-scatter.2.cloned.1.call-update
  503.6 0.3 all-reduce.9.cloned.1.call-start
  503.9 283.5 %reduce-scatter.2.cloned.1.call-done = f32[2,256,1024]{2,1,0:T(8,128)} async-done(((f32[2,8192,1024]{2,1,0:T(8,128)}), f32[2,256,1024]{2,1,0:T(8,128)}) %reduce-scatter.2.cloned.1.call-update) | async-done | bytes 2097168 | tf_op jit(solution)/shard_map/reduce_scatter | solution.py:51
  787.4 2.3 fusion.31
  789.7 1.0 fusion.16
  790.7 0.6 broadcast_add_fusion
  791.4 1.3 copy-done.7
  792.7 2.8 convolution_bitcast_fusion.1
  795.4 0.1 all-reduce.9.cloned.1.call-update
  795.5 65.3 %convolution_bitcast_fusion = f32[1664,1024]{1,0:T(8,128)} fusion(bf16[2,8192,1664]{1,2,0:T(8,128)(2,1)} %fusion.2, bf16[2,8192,1024]{2,1,0:T(8,128)(2,1)} %all-gather.2.cloned.1.call-done), kind=kOutput, calls=%fused_computation.7 | convolution fusion | flops 55834574848 | bytes 94896128 | tf_op jit(solution)/shard_map/hsv,hsd->vd/dot_general | solution.py:49
  860.8 1.2 constant_dynamic-slice_fusion
  862.0 45.3 %all-reduce = (f32[2,1024]{1,0:T(2,128)}, f32[2,1024]{1,0:T(2,128)}) all-reduce(f32[2,1024]{1,0:T(2,128)S(1)} %get-tuple-element.16, f32[2,1024]{1,0:T(2,128)S(1)} %get-tuple-element.18), channel_id=1, replica_groups=mesh['dp'=1,'tp'=32] {'tp'}, use_global_device_ids=true, to_apply=%region_14.15 | all-reduce | flops 4096 | bytes 32768 | tf_op jit(solution)/shard_map/psum | solution.py:56
  907.3 3.1 fusion.19
  910.5 5.5 copy.15
  (40 shorter events, 0.1 us)
Async XLA Ops:
  7.2 119.3 %copy-start = (bf16[1664,1024]{1,0:T(8,128)(2,1)S(1)}, bf16[1664,1024]{1,0:T(8,128)(2,1)}, u32[]{:S(2)}) copy-start(bf16[1664,1024]{1,0:T(8,128)(2,1)} %param.11) | copy-start | bytes 10223620
  7.2 4.6 copy-start.19
  7.2 4.6 copy-start.11
  7.2 119.3 %all-gather.2.cloned.1.call-start = ((), (), s32[]{:S(2)}) async-start(), calls=%async_computation.1 | async-start | bytes 34603008 | tf_op jit(solution)/shard_map/all_gather | solution.py:28
  7.3 2.6 copy-start.2
  9.9 1.3 copy-start.5
  10.2 1.0 copy-start.13
  10.2 3.2 copy-start.20
  10.2 3.2 copy-start.21
  10.6 0.6 copy-start.17
  11.2 0.6 copy-start.15
  13.3 269.5 %all-reduce.5.cloned.1.call-start = ((), (), s32[]{:S(2)}) async-start(), calls=%async_computation.2 | async-start | bytes 131072 | tf_op jit(solution)/shard_map/pmax | solution.py:38
  46.8 0.7 copy-start.10
  192.7 186.2 %all-reduce.7.cloned.1.call-start = ((), (), s32[]{:S(2)}) async-start(), calls=%async_computation.3 | async-start | bytes 262144 | tf_op jit(solution)/shard_map/psum | solution.py:40
  192.8 90.1 %copy-start.9 = (f32[2,8192]{1,0:T(2,128)S(1)}, f32[2,8192]{1,0:T(2,128)}, u32[]{:S(2)}) copy-start(f32[2,8192]{1,0:T(2,128)} %get-tuple-element.26) | copy-start | bytes 196612
  285.4 502.0 %reduce-scatter.2.cloned.1.call-start = ((), (), s32[]{:S(2)}) async-start(), calls=%async_computation.4 | async-start | bytes 69206016 | tf_op jit(solution)/shard_map/reduce_scatter | solution.py:51
  503.5 283.9 %copy-start.3 = (bf16[256,1024]{1,0:T(8,128)(2,1)S(1)}, bf16[256,1024]{1,0:T(8,128)(2,1)}, u32[]{:S(2)}) copy-start(bf16[256,1024]{1,0:T(8,128)(2,1)} %param.7) | copy-start | bytes 1572868
  503.5 283.9 %copy-start.6 = (bf16[1,256,1024]{2,1,0:T(8,128)(2,1)S(1)}, bf16[1,256,1024]{2,1,0:T(8,128)(2,1)}, u32[]{:S(2)}) copy-start(bf16[1,256,1024]{2,1,0:T(8,128)(2,1)} %copy-done.5) | copy-start | bytes 1572868
  503.5 283.9 %copy-start.12 = (f32[2,1024]{1,0:T(2,128)S(1)}, f32[2,1024]{1,0:T(2,128)}, u32[]{:S(2)}) copy-start(f32[2,1024]{1,0:T(2,128)} %param.9) | copy-start | bytes 24580
  503.5 283.9 %copy-start.14 = (f32[2,256]{1,0:T(2,128)S(1)}, f32[2,256]{1,0:T(2,128)}, u32[]{:S(2)}) copy-start(f32[2,256]{1,0:T(2,128)} %copy-done.13) | copy-start | bytes 6148
  503.5 286.2 %copy-start.18 = (f32[2,256]{1,0:T(2,128)S(1)}, f32[2,256]{1,0:T(2,128)}, u32[]{:S(2)}) copy-start(f32[2,256]{1,0:T(2,128)} %copy-done.17) | copy-start | bytes 6148
  503.6 286.2 %copy-start.16 = (f32[2,256]{1,0:T(2,128)S(1)}, f32[2,256]{1,0:T(2,128)}, u32[]{:S(2)}) copy-start(f32[2,256]{1,0:T(2,128)} %copy-done.15) | copy-start | bytes 6148
  503.6 406.9 %all-reduce.9.cloned.1.call-start = ((), (), s32[]{:S(2)}) async-start(), calls=%async_computation.5 | async-start | bytes 8388608 | tf_op jit(solution)/shard_map/psum | solution.py:56
  787.4 2.3 copy-start.4
  791.3 1.3 copy-start.7
  795.5 111.8 %copy-start.8 = (f32[2,256,1024]{2,1,0:T(8,128)S(1)}, f32[2,256,1024]{2,1,0:T(8,128)}, u32[]{:S(2)}) copy-start(f32[2,256,1024]{2,1,0:T(8,128)} %copy-done.7) | copy-start | bytes 6291460
  910.5 5.5 copy-start.1
Sparse Core Ops, SparseCore 0:
  13.4 113.0 all-gather.1
  192.8 89.9 all-reduce.4
  286.7 92.1 all-reduce.6
  503.7 283.6 reduce-scatter.1
  795.6 101.1 all-reduce.8
where the time goes:
time: 923 us; the launch traced here: 922 us
  waiting for transfers between devices  508 us (55%)
  matrix products  209 us (23%)
  other arithmetic  102 us (11%)
  blocking collectives  78.7 us (9%)
  between operations  14.1 us (2%)
  local copies, waits for them, and re-layouts  9.94 us (1%)
    reduce_scatter x1, waiting for transfers between devices, device_step(): dx_loc = lax.psum_scatter(dx_part, 'tp', scatter_dimension=1, tiled=True)  284 us
    psum x1, waiting for transfers between devices, device_step(): glob_stats = lax.psum(part_stats, 'tp')  92.2 us
    all_gather x1, waiting for transfers between devices, device_step(): x_all = lax.all_gather(x_loc, 'tp', axis=1, tiled=True)  79 us
    dot_general x1, matrix products, device_step(): jnp.einsum('hsv,vd->hsd', d_logits, embed, preferred_element_type=jnp.flo...  69.2 us
    dot_general x1, matrix products, device_step(): jnp.einsum('hsd,vd->hsv', x_all, embed, preferred_element_type=jnp.float32)  66.2 us
    dot_general x1, matrix products, device_step(): jnp.einsum('hsv,hsd->vd', d_logits, x_all, preferred_element_type=jnp.flo...  65.3 us
    convert_element_type x1, other arithmetic, device_step(): (jnp.where(is_target, softmax_val - 1.0, softmax_val) * weight[..., None]...  53.1 us
    pmax x1, waiting for transfers between devices, device_step(): glob_max = lax.pmax(local_max, 'tp')  52.5 us
  transfers between devices with their start and end apart: 5, of which 4 were waited for; matrix products, arithmetic and copies ran while one was open for 12% of the time, Pallas kernels for 0%

commit v1 on v0

v1 whole, which is shorter than its diff:
```python
import functools
import math

import jax
import jax.numpy as jnp
from jax import lax
from jax.experimental import pallas as pl
from jax.experimental.pallas import tpu as pltpu
from jax.sharding import PartitionSpec as P

LN_EPS = 1e-5
CORES = 2
SIDE = 4
F32 = jnp.float32
BF16 = jnp.bfloat16
MESH = pl.DeviceIdType.MESH
DIRS = (1, -1)


def guarded(cond, fn):
    if isinstance(cond, bool):
        if cond:
            fn()
    else:
        pl.when(cond)(fn)


def both(a, b):
    return a and b if isinstance(a, bool) else a & b


def layer_norm(values, gain, bias):
    mean_val = jnp.mean(values, axis=-1, keepdims=True)
    centered = values - mean_val
    variance = jnp.mean(centered * centered, axis=-1, keepdims=True)
    return centered * lax.rsqrt(variance + LN_EPS) * gain + bias


def dot(a, b, ca, cb):
    return lax.dot_general(a, b, (((ca,), (cb,)), ((), ())), preferred_element_type=F32)


def fused_kernel(nq, info_ref, hid_ref, w2_ref, gain_ref, bias_ref, emb_ref,
                 dx_out, de_out, loss_out, cnt_out,
                 e_all, d_e, zt, dzt, x_new, x_next, x_cur, h_all, w2, d_x, r1, r2, r3, r4,
                 info_all, tgt_v, wgt_v, msk_v, cnt, stat_s, stat_r, m_v, s_v, lse_l, lse_v, tgt_a, tgt_p, loss_v, loss_p,
                 load_sem, ag_s, ag_r, rs_s, rs_r, st_s, st_r, misc_s, misc_r, free_sem):
    nch = 2 * nq
    rows = emb_ref.shape[0]
    vocab = e_all.shape[0]
    dim = e_all.shape[1]
    half = dim // 2
    quart = dim // 4
    chips, blk = SIDE * SIDE, h_all.shape[3]
    rpc = chips * blk
    me = lax.axis_index('tp')
    core = lax.rem(me, CORES)
    chip = lax.div(me, CORES)
    yy = lax.div(chip, SIDE)
    xx = lax.rem(chip, SIDE)

    def wrap(v):
        return lax.rem(v + 2 * SIDE, SIDE)

    def dev(y, x, c):
        return {'tp': (y * SIDE + x) * CORES + c}

    partner = dev(yy, xx, 1 - core)
    peers = [dev(wrap(yy + dy), wrap(xx + dx), core) for dy in range(SIDE) for dx in range(SIDE) if dy or dx]

    def neighbour(axis, d):
        return dev(yy, wrap(xx + d), core) if axis == 0 else dev(wrap(yy + d), xx, core)

    def remote(src, dst, ssem, rsem, target):
        return pltpu.make_async_remote_copy(src_ref=src, dst_ref=dst, send_sem=ssem, recv_sem=rsem,
                                            device_id=target, device_id_type=MESH)

    my_rows = pl.ds(pl.multiple_of(core * rows, 128), rows)
    other_rows = pl.ds(pl.multiple_of((1 - core) * rows, 128), rows)
    load_e = pltpu.make_async_copy(emb_ref, e_all.at[my_rows], load_sem.at[0])
    load_w = pltpu.make_async_copy(w2_ref, w2, load_sem.at[1])
    load_h = [pltpu.make_async_copy(hid_ref.at[pl.ds(q * blk, blk)], h_all.at[q, yy, xx], load_sem.at[2 + q])
              for q in range(nq)]
    for c in load_h:
        c.start()
    load_e.start()
    load_w.start()

    barrier = pltpu.get_barrier_semaphore()
    for t in peers + [partner]:
        pl.semaphore_signal(barrier, inc=1, device_id=t, device_id_type=MESH)
    pl.semaphore_wait(barrier, len(peers) + 1)

    def line(h, q, pos1, pos2, cols):
        px, py = (pos1, pos2) if h == 0 else (pos2, pos1)
        py = slice(None) if py is None else py
        px = slice(None) if px is None else px
        return h_all.at[q, py, px, :, cols]

    def coords(h):
        return (xx, yy) if h == 0 else (yy, xx)

    def sub(h, d):
        return pl.ds(h * half + (0 if d == 1 else quart), quart)

    def cols_of(h):
        return pl.ds(h * half, half)

    def ag_copy(step, h, q, d):
        a, b = coords(h)
        axis = h if step < 2 else 1 - h
        if step == 0:
            r = line(h, q, a, b, cols_of(h))
        elif step == 1:
            r = line(h, q, wrap(a - d), b, sub(h, d))
        elif step == 2:
            r = line(h, q, None, b, cols_of(h))
        else:
            r = line(h, q, None, wrap(b - d), sub(h, d))
        return remote(r, r, ag_s.at[q, step, h, 0 if d == 1 else 1], ag_r.at[q, step, h, 0 if d == 1 else 1],
                      neighbour(axis, d))

    def ag_start(step, q):
        for h in range(2):
            for d in DIRS:
                ag_copy(step, h, q, d).start()

    def ag_wait_recv(step, q):
        for h in range(2):
            for d in DIRS:
                a, b = coords(h)
                if step == 0:
                    r = line(h, q, wrap(a - d), b, cols_of(h))
                elif step == 1:
                    r = line(h, q, wrap(a - 2 * d), b, sub(h, d))
                elif step == 2:
                    r = line(h, q, None, wrap(b - d), cols_of(h))
                else:
                    r = line(h, q, None, wrap(b - 2 * d), sub(h, d))
                k = 0 if d == 1 else 1
                remote(r, r, ag_s.at[q, step, h, k], ag_r.at[q, step, h, k], partner).wait_recv()

    def ag_tick(k):
        for step in (3, 2, 1, 0):
            q = k - step

            def go(step=step, q=q):
                if step > 0:
                    ag_wait_recv(step - 1, q)
                ag_start(step, q)
            guarded(both(q >= 0, q < nq), go)

    def ag_finish(q):
        ag_wait_recv(3, q)
        for step in range(4):
            for h in range(2):
                for d in DIRS:
                    ag_copy(step, h, q, d).wait_send()

    for c in load_h:
        c.wait()
    ag_tick(0)

    info_copies = [remote(info_ref, info_all.at[chip], misc_s.at[0], misc_r.at[0], t) for t in peers]
    for c in info_copies:
        c.start()
    info_all[chip] = info_ref[...]
    load_e.wait()
    send_e = remote(e_all.at[my_rows], e_all.at[my_rows], misc_s.at[1], misc_r.at[1], partner)
    send_e.start()
    ag_tick(1)
    zt[...] = jnp.zeros(zt.shape, F32)
    d_e[...] = jnp.zeros(d_e.shape, F32)
    ag_tick(2)
    every_info = info_all.at[pl.ds(0, chips - 1)]
    remote(every_info, every_info, misc_s.at[0], misc_r.at[0], partner).wait_recv()
    remote(every_info, every_info, misc_s.at[0], misc_r.at[0], partner).wait_send()
    total = jnp.zeros((8, rpc), F32)
    for q in range(nq):
        got = jnp.concatenate([info_all[o][:, q * blk:(q + 1) * blk] for o in range(chips)], axis=1)
        total = total + got
        for hd in range(2):
            c = (1 - hd) * nq + q
            tgt_v[c] = got[hd:hd + 1].astype(jnp.int32) - chip * vocab
            msk_v[c] = got[2 + hd:3 + hd]
    cnt[0] = jnp.broadcast_to(jnp.sum(total, axis=1, keepdims=True), cnt.shape[1:])
    send_c = remote(cnt.at[0], cnt.at[1], misc_s.at[2], misc_r.at[2], partner)
    send_c.start()
    ag_tick(3)
    send_c.wait()
    counts = cnt[0] + cnt[1]
    for hd in range(2):
        for q in range(nq):
            c = (1 - hd) * nq + q
            wgt_v[c] = msk_v[c] / counts[2 + hd:3 + hd, 0:1]
    load_w.wait()

    def part(slot, h, pos1, pos2, cols):
        px, py = (pos1, pos2) if h == 0 else (pos2, pos1)
        py = slice(None) if py is None else py
        px = slice(None) if px is None else px
        return d_x.at[slot, py, px, :, cols]

    def rs_copy(step, slot, h, d):
        a, b = coords(h)
        k = 0 if d == 1 else 1
        if step == 0:
            src, dst = part(slot, h, wrap(a + 2), None, sub(h, d)), r1.at[slot, h, k]
        elif step == 1:
            src, dst = part(slot, h, wrap(a + d), None, cols_of(h)), r2.at[slot, h, k]
        elif step == 2:
            src, dst = part(slot, h, a, wrap(b + 2), sub(h, d)), r3.at[slot, h, k]
        else:
            src, dst = part(slot, h, a, wrap(b + d), cols_of(h)), r4.at[slot, h, k]
        return remote(src, dst, rs_s.at[slot, step, h, k], rs_r.at[slot, step, h, k],
                      neighbour(h if step < 2 else 1 - h, d))

    def rs_step(step, h, c):
        slot = c % 3 if isinstance(c, int) else lax.rem(c + 3, 3)
        a, b = coords(h)

        def go():
            if step > 0:
                for d in DIRS:
                    rs_copy(step - 1, slot, h, d).wait_recv()
            if step == 1:
                for k, d in enumerate(DIRS):
                    r = part(slot, h, wrap(a + d), None, sub(h, d))
                    r[...] = r[...] + r1[slot, h, k]
            elif step == 2:
                r = part(slot, h, a, None, cols_of(h))
                r[...] = r[...] + r2[slot, h, 0] + r2[slot, h, 1]
            elif step == 3:
                for k, d in enumerate(DIRS):
                    r = part(slot, h, a, wrap(b + d), sub(h, d))
                    r[...] = r[...] + r3[slot, h, k]
            elif step == 4:
                r = part(slot, h, a, b, cols_of(h))
                dx_out[c, :, h * half:(h + 1) * half] = r[...] + r4[slot, h, 0] + r4[slot, h, 1]
            if step < 4:
                for d in DIRS:
                    rs_copy(step, slot, h, d).start()
            else:
                for s in range(4):
                    for d in DIRS:
                        rs_copy(s, slot, h, d).wait_send()
        guarded(both(c >= 0, c < nch), go)

    def stat_copies(par):
        return [remote(stat_s.at[par], stat_r.at[par, chip], st_s.at[par], st_r.at[par], t) for t in peers]

    def stat_send(e):
        par = e % 2 if isinstance(e, int) else lax.rem(e, 2)

        @pl.when(e >= 2)
        def _():
            drain = stat_r.at[par, pl.ds(0, chips - 1)]
            remote(drain, drain, st_s.at[par], st_r.at[par], partner).wait_send()
        stat_s[par, 0:1, :] = lse_l[...]
        stat_s[par, 1:2, :] = tgt_p[...]
        stat_r[par, chip] = stat_s[par]
        for c in stat_copies(par):
            c.start()

    def stat_wait(e):
        par = e % 2 if isinstance(e, int) else lax.rem(e, 2)
        drain = stat_r.at[par, pl.ds(0, chips - 1)]
        remote(drain, drain, st_s.at[par], st_r.at[par], partner).wait_recv()
        got = stat_r[par]
        lse = got[:, 0, :]
        top = jnp.max(lse, axis=0, keepdims=True)
        new_lse = top + jnp.log(jnp.sum(jnp.exp(lse - top), axis=0, keepdims=True))

        def put():
            loss_v[e - 1] = (lse_v[...] - jnp.sum(got[:, 1, :], axis=0, keepdims=True)) * msk_v[e - 1]
        guarded(e >= 1, put)
        lse_v[...] = new_lse

    tile = 256

    def project(q):
        h = h_all[q].reshape(rpc, dim)
        for n0 in range(0, dim, half):
            x_new[:, n0:n0 + half] = dot(h, w2[:, n0:n0 + half], 1, 0).astype(BF16)

    def norm_rows(two, q, lo, hi):
        step, per = 64, blk * SIDE
        hd = 1 if two else 0
        for r in range(lo, hi, step):
            if two:
                val = x_new[r:r + step, :]
            else:
                val = h_all[q, r // per, (r % per) // blk:(r % per + step) // blk].reshape(step, dim)
            val = layer_norm(val.astype(F32), gain_ref[hd:hd + 1, :], bias_ref[hd:hd + 1, :])
            x_new[r:r + step, :] = val.astype(BF16)

    def logits_tile(v0, top):
        z = dot(e_all[v0:v0 + tile, :], x_next[...], 1, 1)
        zt[v0:v0 + tile, :] = z
        return jnp.maximum(top, jnp.max(z.reshape(tile // 8, 8, rpc), axis=0))

    def grad_tile(v0, lse, tgt, wgt, acc):
        z = zt[v0:v0 + tile, :]
        ids = lax.broadcasted_iota(jnp.int32, (tile, rpc), 0)
        hit = ids == tgt - v0
        acc = acc + jnp.sum(jnp.where(hit, z, 0.0).reshape(tile // 8, 8, rpc), axis=0)
        prob = jnp.exp(z - lse)
        dzt[v0:v0 + tile, :] = (jnp.where(hit, prob - 1.0, prob) * wgt).astype(BF16)
        return acc

    n_tiles = vocab // tile
    mid = n_tiles // 2 + 1

    def phase_one(i, lo, hi, with_logits):
        c = jnp.maximum(i, 0)
        lse, tgt, wgt = lse_v[...], tgt_v[c], wgt_v[c]
        top = m_v[...] if lo else jnp.full((8, rpc), -jnp.inf, F32)
        acc = tgt_a[...] if lo else jnp.zeros((8, rpc), F32)
        for j in range(lo, hi):
            acc = grad_tile(j * tile, lse, tgt, wgt, acc)
            if with_logits:
                top = logits_tile(j * tile, top)
        if with_logits:
            m_v[...] = top
        tgt_a[...] = acc
        if hi == n_tiles:
            tgt_p[...] = jnp.sum(acc, axis=0, keepdims=True)

    def dx_half(slot, h):
        val = dot(dzt[...], e_all[:, h * half:(h + 1) * half], 0, 0)
        d_x[slot, :, :, :, h * half:(h + 1) * half] = val.reshape(SIDE, SIDE, blk, half)

    def exp_pass():
        top = jnp.max(m_v[...], axis=0, keepdims=True)
        acc = jnp.zeros((8, rpc), F32)
        for j in range(n_tiles):
            prob = jnp.exp(zt[j * tile:(j + 1) * tile, :] - top)
            acc = acc + jnp.sum(prob.reshape(tile // 8, 8, rpc), axis=0)
        lse_l[...] = top + jnp.log(jnp.sum(acc, axis=0, keepdims=True))

    de_tile = rows // 4

    def phase_three(i, second, with_grad, two, q):
        base = (core if second else 1 - core) * rows
        lo = rpc // 2 if second else 0
        if two:
            if not second:
                project(q)
            else:
                norm_rows(True, q, 0, rpc)
        else:
            norm_rows(False, q, lo, lo + rpc // 2)
        if with_grad:
            for j in range(4):
                r = pl.ds(pl.multiple_of(base + j * de_tile, 32), de_tile)
                d_e[r, :] = d_e[r, :] + dot(dzt[r, :], x_cur[...], 1, 0)

    def three(i, second):
        q = lax.rem(i + 2, nq)
        pl.when(i < 0)(lambda: phase_three(i, second, False, True, q))
        pl.when((i >= 0) & (i < nq - 2))(lambda: phase_three(i, second, True, True, q))
        pl.when(i >= nq - 2)(lambda: phase_three(i, second, True, False, q))

    def give(h):
        lanes = slice(h * half, (h + 1) * half)
        return remote(d_e.at[other_rows, lanes], zt.at[pl.ds(h * rows, rows)], misc_s.at[3 + h], misc_r.at[3 + h], partner)

    m_v[...] = jnp.zeros(m_v.shape, F32)
    lse_v[...] = jnp.zeros(lse_v.shape, F32)
    lse_l[...] = jnp.zeros(lse_l.shape, F32)
    remote(e_all.at[other_rows], e_all.at[other_rows], misc_s.at[1], misc_r.at[1], partner).wait()

    def chunk(i, carry):
        slot = lax.rem(i + 3, 3)
        last = i == nch - 1
        pl.when(i >= 0)(lambda: stat_wait(i))
        pl.when((i >= -1) & (i < nch - 1))(lambda: phase_one(i, 0, mid, True))
        pl.when(last)(lambda: phase_one(i, 0, mid, False))
        rs_step(1, 1, i - 1)
        rs_step(3, 1, i - 2)
        pl.when((i >= -1) & (i < nch - 1))(lambda: phase_one(i, mid, n_tiles, True))
        pl.when(last)(lambda: phase_one(i, mid, n_tiles, False))
        pl.when(last)(lambda: pl.semaphore_signal(free_sem, inc=1, device_id=partner, device_id_type=MESH))
        rs_step(4, 0, i - 2)
        pl.when(i >= -1)(lambda: ag_tick(2 * i + 7))

        @pl.when(i == -1)
        def _():
            exp_pass()

        @pl.when((i >= 0) & (i < nch - 1))
        def _():
            dx_half(slot, 0)
            exp_pass()

        @pl.when(last)
        def _():
            dx_half(slot, 0)
        pl.when(i >= -1)(lambda: stat_send(i + 1))
        rs_step(0, 0, i)
        rs_step(4, 1, i - 2)
        pl.when(i >= 0)(lambda: dx_half(slot, 1))
        rs_step(0, 1, i)
        rs_step(2, 0, i - 1)
        pl.when(i < nq - 2)(lambda: ag_finish(i + 2))
        three(i, False)

        @pl.when(last)
        def _():
            pl.semaphore_wait(free_sem, 1)
            for h in range(2):
                give(h).start()
        rs_step(2, 1, i - 1)
        three(i, True)
        rs_step(1, 0, i)
        rs_step(3, 0, i - 1)
        ag_tick(2 * i + 8)
        x_cur[...] = x_next[...]
        x_next[...] = x_new[...]
        return carry

    lax.fori_loop(-2, nch, chunk, 0)

    c = nch - 1
    rs_step(1, 1, c)
    rs_step(3, 1, c - 1)
    rs_step(4, 0, c - 1)
    rs_step(4, 1, c - 1)
    stat_wait(nch)
    send_l = remote(loss_v, loss_p, misc_s.at[5], misc_r.at[5], partner)
    send_l.start()
    rs_step(2, 0, c)
    rs_step(2, 1, c)
    for h in range(2):
        give(h).wait()
    outs = []
    out_tile = rows // 8
    for j in range(8):
        r = pl.ds(pl.multiple_of(core * rows + j * out_tile, 8), out_tile)
        for h in range(2):
            lanes = slice(h * half, (h + 1) * half)
            d_e[r, lanes] = d_e[r, lanes] + zt[h * rows + j * out_tile:h * rows + (j + 1) * out_tile, :]
        outs.append(pltpu.make_async_copy(d_e.at[r], de_out.at[pl.ds(j * out_tile, out_tile)], load_sem.at[j]))
        outs[-1].start()
    rs_step(3, 0, c)
    rs_step(3, 1, c)
    send_l.wait()
    loss_out[core] = loss_v[...]
    loss_out[1 - core] = loss_p[...]
    cnt_out[...] = counts
    for par in range(2):
        drain = stat_r.at[par, pl.ds(0, chips - 1)]
        remote(drain, drain, st_s.at[par], st_r.at[par], partner).wait_send()
    rs_step(4, 0, c)
    rs_step(4, 1, c)
    for o in outs:
        o.wait()


def solution(mesh):
    tok_spec = P(('dp', 'tp'), None)
    row_spec = P(None, ('dp', 'tp'))
    chips = mesh.shape['tp'] // CORES
    assert math.isqrt(chips) == SIDE

    def run_kernel(info, hidden, w_two, gain, bias, embed):
        tok, dim = hidden.shape
        rows = embed.shape[0]
        blk = 32
        nq = tok // blk
        nch, rpc, half, quart = 2 * nq, chips * blk, dim // 2, dim // 4
        vocab = CORES * rows
        vmem = pl.BlockSpec(memory_space=pltpu.VMEM)
        hbm = pl.BlockSpec(memory_space=pltpu.MemorySpace.HBM)
        dma = pltpu.SemaphoreType.DMA
        return pl.pallas_call(
            functools.partial(fused_kernel, nq),
            out_shape=(jax.ShapeDtypeStruct((nch, blk, dim), F32), jax.ShapeDtypeStruct((rows, dim), F32),
                       jax.ShapeDtypeStruct((CORES, nch, 1, rpc), F32), jax.ShapeDtypeStruct((8, 128), F32)),
            in_specs=[vmem, hbm, hbm, vmem, vmem, hbm],
            out_specs=[vmem, hbm, vmem, vmem],
            scratch_shapes=[
                pltpu.VMEM((vocab, dim), BF16), pltpu.VMEM((vocab, dim), F32),
                pltpu.VMEM((vocab, rpc), F32), pltpu.VMEM((vocab, rpc), BF16),
                pltpu.VMEM((rpc, dim), BF16), pltpu.VMEM((rpc, dim), BF16), pltpu.VMEM((rpc, dim), BF16),
                pltpu.VMEM((nq, SIDE, SIDE, blk, dim), BF16), pltpu.VMEM((dim, dim), BF16),
                pltpu.VMEM((3, SIDE, SIDE, blk, dim), F32),
                pltpu.VMEM((3, 2, 2, SIDE, blk, quart), F32), pltpu.VMEM((3, 2, 2, SIDE, blk, half), F32),
                pltpu.VMEM((3, 2, 2, blk, quart), F32), pltpu.VMEM((3, 2, 2, blk, half), F32),
                pltpu.VMEM((chips, 8, tok), F32), pltpu.VMEM((nch, 1, rpc), jnp.int32),
                pltpu.VMEM((nch, 1, rpc), F32), pltpu.VMEM((nch, 1, rpc), F32), pltpu.VMEM((2, 8, 128), F32),
                pltpu.VMEM((2, 2, rpc), F32), pltpu.VMEM((2, chips, 2, rpc), F32),
                pltpu.VMEM((8, rpc), F32), pltpu.VMEM((8, rpc), F32), pltpu.VMEM((1, rpc), F32),
                pltpu.VMEM((1, rpc), F32), pltpu.VMEM((8, rpc), F32), pltpu.VMEM((1, rpc), F32),
                pltpu.VMEM((nch, 1, rpc), F32), pltpu.VMEM((nch, 1, rpc), F32),
                dma((2 + nq,)), dma((nq, 4, 2, 2)), dma((nq, 4, 2, 2)), dma((3, 4, 2, 2)), dma((3, 4, 2, 2)),
                dma((2,)), dma((2,)), dma((6,)), dma((6,)), pltpu.SemaphoreType.REGULAR,
            ],
            compiler_params=pltpu.CompilerParams(collective_id=0, has_side_effects=True,
                                                 vmem_limit_bytes=63 * 1024 * 1024),
            name='fused_heads',
        )(info, hidden, w_two, gain, bias, embed)

    def device_step(hidden, w_two, ln_scale, ln_shift, embed, targets, loss_mask):
        tok, dim = hidden.shape
        me = lax.axis_index('tp')
        info = jnp.concatenate([targets, loss_mask, jnp.zeros((4, tok), jnp.int32)]).astype(F32)
        dx, d_embed, losses, counts = run_kernel(info, hidden, w_two, ln_scale, ln_shift, embed)
        dx_loc = dx.reshape(2, tok, dim)[::-1]
        losses = losses.reshape(CORES, 2, tok // 32, chips, 32)[:, ::-1]
        mine = lax.dynamic_index_in_dim(losses, me % CORES, 0, keepdims=False)
        token_loss = lax.dynamic_index_in_dim(mine, me // CORES, 2, keepdims=False).reshape(2, tok)
        total_loss = jnp.sum(jnp.sum(losses, axis=(0, 2, 3, 4)) / counts[2:4, 0]).reshape(1)
        proj_out = jnp.dot(hidden, w_two, preferred_element_type=F32).astype(BF16)
        norm_input = jnp.stack([hidden.astype(F32), proj_out.astype(F32)])
        _, ln_back = jax.vjp(jax.vmap(layer_norm), norm_input, ln_scale, ln_shift)
        d_norm_in, d_scale_part, d_shift_part = ln_back(dx_loc)
        d_proj = d_norm_in[1].astype(BF16)
        d_hidden = (d_norm_in[0] + jnp.einsum('td,ed->te', d_proj, w_two, preferred_element_type=F32)).astype(BF16)
        d_w_part = jnp.einsum('te,td->ed', hidden, d_proj, preferred_element_type=F32)
        d_w_two, d_scale, d_shift = lax.psum((d_w_part, d_scale_part, d_shift_part), 'tp')
        return token_loss, total_loss, d_hidden, d_embed, d_w_two, d_scale, d_shift

    return jax.shard_map(device_step, mesh=mesh,
                         in_specs=(tok_spec, P(), P(), P(), P('tp', None), row_spec, row_spec),
                         out_specs=(row_spec, P('dp'), tok_spec, tok_spec, P('dp', None), P('dp', None), P('dp', None)),
                         check_vma=False)
```

time: 923 us -> 477 us (0.52)
  waiting for transfers between devices: 508 us -> 49.5 us
  Pallas kernels: 0 us -> 336 us
  matrix products: 209 us -> 8.39 us
  other arithmetic: 102 us -> 6.14 us
  blocking collectives: 78.7 us -> 46.9 us
    pallas_call x0 -> x1, Pallas kernels: none -> 336 us  [run_kernel(): pl.pallas_call(functools.partial(fused_kernel, nq), out_shape=(jax.ShapeD...]
    reduce_scatter x1 -> x0, waiting for transfers between devices: 284 us -> none  [device_step(): dx_loc = lax.psum_scatter(dx_part, 'tp', scatter_dimension=1, tiled=True)]
    dot_general x6 -> x3, matrix products: 209 us -> 8.39 us  [the longest x1 3.14 us: device_step(): jnp.einsum('td,ed->te', d_proj, w_two, preferred_element_type=F32)]
    psum x1 -> x0, waiting for transfers between devices: 92.2 us -> none  [device_step(): glob_stats = lax.psum(part_stats, 'tp')]
    all_gather x1 -> x0, waiting for transfers between devices: 79 us -> none  [device_step(): x_all = lax.all_gather(x_loc, 'tp', axis=1, tiled=True)]
    convert_element_type x2 -> x1, other arithmetic: 54.5 us -> 0.67 us  [device_step(): jnp.concatenate([targets, loss_mask, jnp.zeros((4, tok), jnp.int32)])]
    pmax x1 -> x0, waiting for transfers between devices: 52.5 us -> none  [device_step(): glob_max = lax.pmax(local_max, 'tp')]
    psum x1, waiting for transfers between devices: 0.01 us -> 49.4 us  [device_step(): lax.psum((d_w_part, d_scale_part, d_shift_part), 'tp')]
  transfers between devices with their start and end apart: 5 -> 1, of which waited for: 4 -> 1; matrix products, arithmetic and copies ran while one was open for 12% -> 1% of each run, Pallas kernels for 0% -> 0%
where the time goes in v1:
time: 477 us
  Pallas kernels  336 us (70%)
  waiting for transfers between devices  49.5 us (10%)
  blocking collectives  46.9 us (10%)
  local copies, waits for them, and re-layouts  15.4 us (3%)
  between operations  14.6 us (3%)
  matrix products  8.39 us (2%)
  other arithmetic  6.14 us (1%)
    pallas_call x1, Pallas kernels, run_kernel(): pl.pallas_call(functools.partial(fused_kernel, nq), out_shape=(jax.ShapeD...  336 us
    psum x1, waiting for transfers between devices, device_step(): lax.psum((d_w_part, d_scale_part, d_shift_part), 'tp')  49.4 us
    psum x1, blocking collectives, device_step(): lax.psum((d_w_part, d_scale_part, d_shift_part), 'tp')  46.9 us
    unnamed x20, local copies, waits for them, and re-layouts  13.8 us
  transfers between devices with their start and end apart: 1, of which 1 were waited for; matrix products, arithmetic and copies ran while one was open for 1% of the time, Pallas kernels for 0%

profile of v1, /device:TPU:97, one launch (start us, length us, event | category | flops | bytes accessed | tf_op | source)
XLA Modules:
  0.0 476.5 jit_solution(17528608224786994186)
XLA Ops:
  7.2 0.0 copy-start.1
  7.2 0.1 all-reduce.3.cloned.1.call-start
  7.3 0.1 pad.4.clone
  7.3 0.0 copy-start.7
  7.3 0.0 copy-start.8
  7.3 2.5 fusion.9
  9.9 0.0 copy-start.3
  9.9 0.0 copy-done.1
  9.9 0.2 convert_reduce_fusion
  10.1 0.6 copy-done.3
  10.6 0.0 copy-done.7
  10.7 0.0 copy-done.8
  10.7 0.7 add_convert_fusion.info_ref
  11.3 0.0 copy-start.2
  11.3 0.0 copy-start.5
  11.3 335.5 %fused_heads.1 = (f32[16,32,1024]{2,1,0:T(8,128)}, f32[1664,1024]{1,0:T(8,128)}, f32[2,16,1,512]{3,2,1,0:T(1,128)}, f32[8,128]{1,0:T(8,128)}) custom-call(f32[8,256]{1,0:T(8,128)} %add_convert_fusion.info_ref, bf16[256,1024]{1,0:T(8,128)(2,1)} %hid_ref.1, bf16[1024,1024]{1,0:T(8,128)(2,1)} %w2_ref.1, f32[2,1024]{1,0:T(2,128)} %gain_ref.1, ...), custom_call_target="tpu_custom_call" | custom-call | tf_op jit(solution)/shard_map/fused_heads/pallas_call | solution.py:476
  346.8 0.0 copy-start
  346.9 0.0 copy-start.4
  346.9 0.0 copy-done.2
  346.9 0.0 copy-done.5
  346.9 2.5 fusion.4
  349.5 0.0 copy-done
  349.5 0.0 copy-done.4
  349.5 1.1 fusion.7
  350.6 0.6 broadcast_add_fusion
  351.3 2.8 convolution_bitcast_fusion
  354.0 0.0 copy-start.6
  354.0 0.1 all-reduce.3.cloned.1.call-update
  354.1 0.8 copy-done.6
  354.9 0.2 reduce
  355.0 0.1 reshape.61
  355.3 0.7 reshape.62
  355.9 0.1 reverse_reduce_fusion.1
  356.0 46.9 %all-reduce = (f32[2,1024]{1,0:T(2,128)}, f32[2,1024]{1,0:T(2,128)}) all-reduce(f32[2,1024]{1,0:T(2,128)S(1)} %get-tuple-element.29, f32[2,1024]{1,0:T(2,128)S(1)} %get-tuple-element.31), channel_id=1, replica_groups=mesh['dp'=1,'tp'=32] {'tp'}, use_global_device_ids=true, to_apply=%region_8.9 | all-reduce | flops 4096 | bytes 32768 | tf_op jit(solution)/shard_map/psum | solution.py:521
  402.9 0.8 slice_reduce_fusion
  403.7 0.6 divide_reduce_fusion
  404.3 3.1 fusion.8
  407.4 49.4 %all-reduce.3.cloned.1.call-done = f32[1024,1024]{0,1:T(8,128)} async-done(((f32[1024,1024]{0,1:T(8,128)}), f32[1024,1024]{0,1:T(8,128)}) %all-reduce.3.cloned.1.call-update) | async-done | bytes 4194320 | tf_op jit(solution)/shard_map/psum | solution.py:521
  456.9 5.3 %copy.15 = f32[1024,1024]{1,0:T(8,128)} copy(f32[1024,1024]{0,1:T(8,128)} %all-reduce.3.cloned.1.call-done) | data formatting | bytes 8388608
  462.2 7.1 %copy.18 = f32[1664,1024]{1,0:T(8,128)} copy(f32[1664,1024]{1,0:T(8,128)} %get-tuple-element.48) | data formatting | bytes 13631488
  (6 shorter events, 0.1 us)
Async XLA Ops:
  7.2 2.7 copy-start.1
  7.2 449.7 %all-reduce.3.cloned.1.call-start = ((), (), s32[]{:S(2)}) async-start(), calls=%async_computation | async-start | bytes 8388608 | tf_op jit(solution)/shard_map/psum | solution.py:521
  7.3 3.3 copy-start.7
  7.3 3.3 copy-start.8
  9.9 0.8 copy-start.3
  11.3 335.5 %copy-start.2 = (bf16[256,1024]{1,0:T(8,128)(2,1)S(1)}, bf16[256,1024]{1,0:T(8,128)(2,1)}, u32[]{:S(2)}) copy-start(bf16[256,1024]{1,0:T(8,128)(2,1)} %hid_ref.1) | copy-start | bytes 1572868
  11.3 335.6 %copy-start.5 = (f32[2,1024]{1,0:T(2,128)S(1)}, f32[2,1024]{1,0:T(2,128)}, u32[]{:S(2)}) copy-start(f32[2,1024]{1,0:T(2,128)} %gain_ref.1) | copy-start | bytes 24580
  346.8 2.6 copy-start
  346.9 2.6 copy-start.4
  354.0 0.8 copy-start.6
Sparse Core Ops, SparseCore 0:
  354.2 102.5 all-reduce.2

commit v2 on v1

v2 whole, which is shorter than its diff:
```python
import functools
import math

import jax
import jax.numpy as jnp
from jax import lax
from jax.experimental import pallas as pl
from jax.experimental.pallas import tpu as pltpu
from jax.sharding import PartitionSpec as P

LN_EPS = 1e-5
BIG = 1e30
CORES = 2
SIDE = 4
BLOCK = 32
VMEM_BYTES = 67043328
F32 = jnp.float32
BF16 = jnp.bfloat16
MESH = pl.DeviceIdType.MESH
DIRS = (1, -1)


def guarded(cond, fn):
    if isinstance(cond, bool):
        if cond:
            fn()
    else:
        pl.when(cond)(fn)


def both(a, b):
    return a and b if isinstance(a, bool) else a & b


def layer_norm(values, gain, bias):
    mean_val = jnp.mean(values, axis=-1, keepdims=True)
    centered = values - mean_val
    variance = jnp.mean(centered * centered, axis=-1, keepdims=True)
    return centered * lax.rsqrt(variance + LN_EPS) * gain + bias


def dot(a, b, ca, cb):
    return lax.dot_general(a, b, (((ca,), (cb,)), ((), ())), preferred_element_type=F32)


def fused_kernel(nq, info_ref, hid_ref, w2_ref, gain_ref, bias_ref, emb_ref,
                 dh_out, de_out, dw_out, hop, ln_out, loss_out, cnt_out,
                 e_all, d_e, zt, dzt, x_new, x_next, x_cur, h_all, w2, d_x, r1, r2, r3, r4,
                 info_all, tgt_v, wgt_v, msk_v, cnt, stat_s, stat_r, m_v, lse_l, lse_v, tgt_l, loss_v, loss_p,
                 dx_own, dw_part, dw_own, ln_s, ln_r, ln_p,
                 load_sem, ag_s, ag_r, rs_s, rs_r, st_s, st_r, misc_s, misc_r, lx_s, lx_r, wg_s, wg_r, free_sem):
    nch = 2 * nq
    rows = emb_ref.shape[0]
    vocab = e_all.shape[0]
    dim = e_all.shape[1]
    half = dim // 2
    quart = dim // 4
    chips, blk = SIDE * SIDE, h_all.shape[3]
    tok = nq * blk
    extra = nq + 2
    rpc = chips * blk
    me = lax.axis_index('tp')
    core = lax.rem(me, CORES)
    chip = lax.div(me, CORES)
    yy = lax.div(chip, SIDE)
    xx = lax.rem(chip, SIDE)

    def wrap(v):
        return lax.rem(v + 2 * SIDE, SIDE)

    def dev(y, x, c):
        return {'tp': (y * SIDE + x) * CORES + c}

    partner = dev(yy, xx, 1 - core)
    peers = [dev(wrap(yy + dy), wrap(xx + dx), core) for dy in range(SIDE) for dx in range(SIDE) if dy or dx]

    def neighbour(axis, d):
        return dev(yy, wrap(xx + d), core) if axis == 0 else dev(wrap(yy + d), xx, core)

    def remote(src, dst, ssem, rsem, target):
        return pltpu.make_async_remote_copy(src_ref=src, dst_ref=dst, send_sem=ssem, recv_sem=rsem,
                                            device_id=target, device_id_type=MESH)

    my_rows = pl.ds(pl.multiple_of(core * rows, 128), rows)
    other_rows = pl.ds(pl.multiple_of((1 - core) * rows, 128), rows)
    load_e = pltpu.make_async_copy(emb_ref, e_all.at[my_rows], load_sem.at[0])
    load_w = pltpu.make_async_copy(w2_ref, w2, load_sem.at[1])
    load_h = [pltpu.make_async_copy(hid_ref.at[pl.ds(q * blk, blk)], h_all.at[q, yy, xx], load_sem.at[2 + q])
              for q in range(nq)]
    for c in load_h:
        c.start()
    load_e.start()
    load_w.start()

    barrier = pltpu.get_barrier_semaphore()
    for t in peers + [partner]:
        pl.semaphore_signal(barrier, inc=1, device_id=t, device_id_type=MESH)
    pl.semaphore_wait(barrier, len(peers) + 1)

    def coords(h):
        return (xx, yy) if h == 0 else (yy, xx)

    def sub(h, d):
        return pl.ds(h * half + (0 if d == 1 else quart), quart)

    def cols_of(h):
        return pl.ds(h * half, half)

    def gathered(buf, step, h, d, back):
        a, b = coords(h)
        if step == 0:
            pos, cols = (wrap(a - back * d), b), cols_of(h)
        elif step == 1:
            pos, cols = (wrap(a - (1 + back) * d), b), sub(h, d)
        elif step == 2:
            pos, cols = (None, wrap(b - back * d)), cols_of(h)
        else:
            pos, cols = (None, wrap(b - (1 + back) * d)), sub(h, d)
        px, py = pos if h == 0 else pos[::-1]
        py = slice(None) if py is None else py
        px = slice(None) if px is None else px
        return buf.at[py, px, :, cols]

    def ag_copy(step, h, q, d, back=0):
        k = 0 if d == 1 else 1
        r = gathered(h_all.at[q], step, h, d, back)
        return remote(r, r, ag_s.at[q, step, h, k], ag_r.at[q, step, h, k],
                      neighbour(h if step < 2 else 1 - h, d))

    def ag_start(step, q):
        for h in range(2):
            for d in DIRS:
                ag_copy(step, h, q, d).start()

    def ag_wait_recv(step, q):
        for h in range(2):
            for d in DIRS:
                ag_copy(step, h, q, d, 1).wait_recv()

    def ag_tick(k):
        for step in (3, 2, 1, 0):
            q = k - step

            def go(step=step, q=q):
                if step > 0:
                    ag_wait_recv(step - 1, q)
                ag_start(step, q)
            guarded(both(q >= 0, q < nq), go)

    def ag_finish(q):
        ag_wait_recv(3, q)
        for step in range(4):
            for h in range(2):
                for d in DIRS:
                    ag_copy(step, h, q, d).wait_send()

    for c in load_h:
        c.wait()
    ag_tick(0)

    info_copies = [remote(info_ref, info_all.at[chip], misc_s.at[0], misc_r.at[0], t) for t in peers]
    for c in info_copies:
        c.start()
    info_all[chip] = info_ref[...]
    load_e.wait()
    send_e = remote(e_all.at[my_rows], e_all.at[my_rows], misc_s.at[1], misc_r.at[1], partner)
    send_e.start()
    ag_tick(1)
    ag_tick(2)
    every_info = info_all.at[pl.ds(0, chips - 1)]
    remote(every_info, every_info, misc_s.at[0], misc_r.at[0], partner).wait_recv()
    remote(every_info, every_info, misc_s.at[0], misc_r.at[0], partner).wait_send()
    total = jnp.zeros((8, rpc), F32)
    for q in range(nq):
        got = jnp.concatenate([info_all[o][:, q * blk:(q + 1) * blk] for o in range(chips)], axis=1)
        total = total + got
        for hd in range(2):
            c = (1 - hd) * nq + q
            tgt_v[c] = got[hd:hd + 1].astype(jnp.int32) - chip * vocab
            msk_v[c] = got[2 + hd:3 + hd]
    cnt[0] = jnp.broadcast_to(jnp.sum(total, axis=1, keepdims=True), cnt.shape[1:])
    send_c = remote(cnt.at[0], cnt.at[1], misc_s.at[2], misc_r.at[2], partner)
    send_c.start()
    ag_tick(3)
    send_c.wait()
    counts = cnt[0] + cnt[1]
    for hd in range(2):
        for q in range(nq):
            c = (1 - hd) * nq + q
            wgt_v[c] = msk_v[c] / counts[2 + hd:3 + hd, 0:1]
    load_w.wait()

    def part(slot, h, pos1, pos2, cols):
        px, py = (pos1, pos2) if h == 0 else (pos2, pos1)
        py = slice(None) if py is None else py
        px = slice(None) if px is None else px
        return d_x.at[slot, py, px, :, cols]

    def rs_copy(step, slot, h, d):
        a, b = coords(h)
        k = 0 if d == 1 else 1
        if step == 0:
            src, dst = part(slot, h, wrap(a + 2), None, sub(h, d)), r1.at[slot, h, k]
        elif step == 1:
            src, dst = part(slot, h, wrap(a + d), None, cols_of(h)), r2.at[slot, h, k]
        elif step == 2:
            src, dst = part(slot, h, a, wrap(b + 2), sub(h, d)), r3.at[slot, h, k]
        else:
            src, dst = part(slot, h, a, wrap(b + d), cols_of(h)), r4.at[slot, h, k]
        return remote(src, dst, rs_s.at[slot, step, h, k], rs_r.at[slot, step, h, k],
                      neighbour(h if step < 2 else 1 - h, d))

    def rs_step(step, h, c):
        slot = c % 3 if isinstance(c, int) else lax.rem(c + 3, 3)
        a, b = coords(h)

        def go():
            if step > 0:
                for d in DIRS:
                    rs_copy(step - 1, slot, h, d).wait_recv()
            if step == 1:
                for k, d in enumerate(DIRS):
                    r = part(slot, h, wrap(a + d), None, sub(h, d))
                    r[...] = r[...] + r1[slot, h, k]
            elif step == 2:
                r = part(slot, h, a, None, cols_of(h))
                r[...] = r[...] + r2[slot, h, 0] + r2[slot, h, 1]
            elif step == 3:
                for k, d in enumerate(DIRS):
                    r = part(slot, h, a, wrap(b + d), sub(h, d))
                    r[...] = r[...] + r3[slot, h, k]
            elif step == 4:
                r = part(slot, h, a, b, cols_of(h))
                val = r[...] + r4[slot, h, 0] + r4[slot, h, 1]

                def keep_dx():
                    at = c - 1 if isinstance(c, int) else jnp.where(c < extra, c, c - 1)
                    dx_own[at, :, h * half:(h + 1) * half] = val

                def keep_dw():
                    dw_own[:, h * half:(h + 1) * half] = val
                guarded(c != extra, keep_dx)
                guarded(c == extra, keep_dw)
            if step < 4:
                for d in DIRS:
                    rs_copy(step, slot, h, d).start()
            else:
                for s in range(4):
                    for d in DIRS:
                        rs_copy(s, slot, h, d).wait_send()
        guarded(both(c >= 0, c <= nch), go)

    def stat_drain(par):
        drain = stat_r.at[par, pl.ds(0, chips - 1)]
        return remote(drain, drain, st_s.at[par], st_r.at[par], partner)

    def stat_send(e):
        par = lax.rem(e, 2)
        pl.when(e >= 2)(lambda: stat_drain(par).wait_send())
        stat_s[par, 0:1, :] = lse_l[...]
        stat_s[par, 1:2, :] = tgt_l[...]
        stat_r[par, chip] = stat_s[par]
        for t in peers:
            remote(stat_s.at[par], stat_r.at[par, chip], st_s.at[par], st_r.at[par], t).start()

    def stat_wait(e):
        par = lax.rem(e, 2)
        stat_drain(par).wait_recv()
        got = stat_r[par]
        lse = got[:, 0, :]
        top = jnp.max(lse, axis=0, keepdims=True)
        lse = top + jnp.log(jnp.sum(jnp.exp(lse - top), axis=0, keepdims=True))
        loss_v[e] = (lse - jnp.sum(got[:, 1, :], axis=0, keepdims=True)) * msk_v[e]
        wgt = wgt_v[e]
        live = wgt > 0.0
        lse_v[...] = jnp.where(live, lse - jnp.log(jnp.where(live, wgt, 1.0)), BIG)

    tile = 256

    def project(q):
        h = h_all[q].reshape(rpc, dim)
        for n0 in range(0, dim, half):
            x_new[:, n0:n0 + half] = dot(h, w2[:, n0:n0 + half], 1, 0).astype(BF16)

    def norm_rows(two, q, lo, hi):
        step, per = 64, blk * SIDE
        hd = 1 if two else 0
        for r in range(lo, hi, step):
            if two:
                val = x_new[r:r + step, :]
            else:
                val = h_all[q, r // per, (r % per) // blk:(r % per + step) // blk].reshape(step, dim)
            val = layer_norm(val.astype(F32), gain_ref[hd:hd + 1, :], bias_ref[hd:hd + 1, :])
            x_new[r:r + step, :] = val.astype(BF16)

    def logits_tile(v0, top):
        z = dot(e_all[v0:v0 + tile, :], x_next[...], 1, 1)
        zt[v0:v0 + tile, :] = z
        return jnp.maximum(top, jnp.max(z.reshape(tile // 8, 8, rpc), axis=0))

    def grad_tile(v0, shift, tgt, wgt):
        prob = jnp.exp(zt[v0:v0 + tile, :] - shift)
        hit = lax.broadcasted_iota(jnp.int32, (tile, rpc), 0) == tgt - v0
        dzt[v0:v0 + tile, :] = jnp.where(hit, prob - wgt, prob).astype(BF16)

    n_tiles = vocab // tile
    mid = n_tiles // 2 + 1

    def phase_one(c, lo, hi, with_logits):
        at = jnp.maximum(c, 0)
        shift, tgt, wgt = lse_v[...], tgt_v[at], wgt_v[at]
        top = m_v[...] if lo else jnp.full((8, rpc), -jnp.inf, F32)
        for j in range(lo, hi):
            grad_tile(j * tile, shift, tgt, wgt)
            if with_logits:
                top = logits_tile(j * tile, top)
        if with_logits:
            m_v[...] = top

    def dx_half(slot, h):
        val = dot(dzt[...], e_all[:, h * half:(h + 1) * half], 0, 0)
        d_x[slot, :, :, :, h * half:(h + 1) * half] = val.reshape(SIDE, SIDE, blk, half)

    def exp_pass(c, slot, with_dx):
        top = jnp.max(m_v[...], axis=0, keepdims=True)
        tgt = tgt_v[c + 1]
        acc = jnp.zeros((8, rpc), F32)
        found = jnp.zeros((8, rpc), F32)
        for j in range(n_tiles):
            if with_dx and j == 9:
                dx_half(slot, 0)
            z = zt[j * tile:(j + 1) * tile, :]
            hit = lax.broadcasted_iota(jnp.int32, (tile, rpc), 0) == tgt - j * tile
            acc = acc + jnp.sum(jnp.exp(z - top).reshape(tile // 8, 8, rpc), axis=0)
            for k in range(0, tile, 8):
                found = jnp.where(hit[k:k + 8], z[k:k + 8], found)
        lse_l[...] = top + jnp.log(jnp.sum(acc, axis=0, keepdims=True))
        tgt_l[...] = jnp.sum(found, axis=0, keepdims=True)

    de_tile = rows // 4

    def phase_three(second, with_grad, two, q):
        base = (core if second else 1 - core) * rows
        lo = rpc // 2 if second else 0
        if not with_grad:
            if not second:
                project(q)
            norm_rows(two, q, lo, lo + rpc // 2)
            return
        for j in range(4):
            norm_rows(two, q, lo + j * rpc // 8, lo + (j + 1) * rpc // 8)
            r = pl.ds(pl.multiple_of(base + j * de_tile, 32), de_tile)
            d_e[r, :] = d_e[r, :] + dot(dzt[r, :], x_cur[...], 1, 0)

    def three(c, second):
        q = lax.rem(c + 2, nq)
        pl.when((c >= -2) & (c < 0))(lambda: phase_three(second, False, True, q))
        if second:
            @pl.when(c == -1)
            def _():
                d_e[...] = jnp.zeros(d_e.shape, F32)
        pl.when((c >= 0) & (c < nq - 2))(lambda: phase_three(second, True, True, q))
        pl.when(c >= nq - 2)(lambda: phase_three(second, True, False, q))

    def own_hidden(j, n, lanes=slice(None)):
        return h_all[j:j + n, yy, xx, :, lanes].reshape(n * blk, -1)

    def norm_back(hd):
        step = 2 * blk
        d_gain = jnp.zeros((8, dim), F32)
        d_bias = jnp.zeros((8, dim), F32)
        if hd == 1:
            for n0 in range(0, dim, half):
                x_new[0:tok, n0:n0 + half] = dot(own_hidden(0, nq), w2[:, n0:n0 + half], 1, 0).astype(BF16)
        for j in range(nq // 2):
            r = j * step
            val = (x_new[r:r + step, :] if hd == 1 else own_hidden(2 * j, 2)).astype(F32)
            cen = val - jnp.mean(val, axis=-1, keepdims=True)
            rstd = lax.rsqrt(jnp.mean(cen * cen, axis=-1, keepdims=True) + LN_EPS)
            hat = cen * rstd
            at = (1 - hd) * nq + 2 * j
            d_y = dx_own[at:at + 2].reshape(step, dim)
            d_gain = d_gain + jnp.sum((d_y * hat).reshape(step // 8, 8, dim), axis=0)
            d_bias = d_bias + jnp.sum(d_y.reshape(step // 8, 8, dim), axis=0)
            g = d_y * gain_ref[hd:hd + 1, :]
            d_in = rstd * (g - jnp.mean(g, axis=-1, keepdims=True) - hat * jnp.mean(g * hat, axis=-1, keepdims=True))
            if hd == 1:
                x_new[tok + r:tok + r + step, :] = d_in.astype(BF16)
            else:
                x_new[r:r + step, :] = (d_in + dx_own[2 * j:2 * j + 2].reshape(step, dim)).astype(BF16)
        ln_s[hd, 0:1, :] = jnp.sum(d_gain, axis=0, keepdims=True)
        ln_s[hd, 1:2, :] = jnp.sum(d_bias, axis=0, keepdims=True)
        ln_r[hd, chip] = ln_s[hd]
        for t in peers:
            remote(ln_s.at[hd], ln_r.at[hd, chip], lx_s.at[hd], lx_r.at[hd], t).start()

    def norm_drain(hd):
        drain = ln_r.at[hd, pl.ds(0, chips - 1)]
        return remote(drain, drain, lx_s.at[hd], lx_r.at[hd], partner)

    send_hop = remote(dw_part, hop, misc_s.at[6], misc_r.at[6], partner)
    load_hop = pltpu.make_async_copy(hop, dw_part, load_sem.at[0])

    def dw_half(k):
        lanes = pl.ds(pl.multiple_of(k * half, half), half)
        return dot(own_hidden(0, nq, lanes), x_new[tok:2 * tok, :], 0, 0).reshape(SIDE, SIDE, blk, dim)

    def dw_begin():
        dw_part[...] = dw_half(1 - core)
        send_hop.start()
        d_x[extra % 3] = dw_half(core)
        dx_own[0:nq] = dot(x_new[tok:2 * tok, :], w2[...], 1, 1).reshape(nq, blk, dim)

    def dw_join():
        send_hop.wait()
        load_hop.start()
        load_hop.wait()
        d_x[extra % 3] = d_x[extra % 3] + dw_part[...]

    dw_mine = dw_out.at[core]
    save_dw = pltpu.make_async_copy(dw_own, dw_out.at[core, yy, xx], load_sem.at[1])
    send_dw = remote(dw_mine, dw_mine, misc_s.at[7], misc_r.at[7], partner)
    dw_other = dw_out.at[1 - core]

    def wg_copy(step, h, d, back=0):
        k = 0 if d == 1 else 1
        r = gathered(dw_mine, step, h, d, back)
        src = dw_own.at[:, cols_of(h)] if step == 0 and not back else r
        return remote(src, r, wg_s.at[step, h, k], wg_r.at[step, h, k], neighbour(h if step < 2 else 1 - h, d))

    def dw_gather(step):
        if step == 0:
            save_dw.start()
        else:
            for h in range(2):
                for d in DIRS:
                    wg_copy(step - 1, h, d, 1).wait_recv()
        if step == 2:
            save_dw.wait()
        if step == 4:
            send_dw.start()
            return
        for h in range(2):
            for d in DIRS:
                wg_copy(step, h, d).start()

    def give(h):
        lanes = slice(h * half, (h + 1) * half)
        return remote(d_e.at[other_rows, lanes], zt.at[pl.ds(h * rows, rows)], misc_s.at[3 + h], misc_r.at[3 + h], partner)

    m_v[...] = jnp.zeros(m_v.shape, F32)
    lse_v[...] = jnp.zeros(lse_v.shape, F32)
    remote(e_all.at[other_rows], e_all.at[other_rows], misc_s.at[1], misc_r.at[1], partner).wait()

    def item(s, carry):
        slot = lax.rem(s + 3, 3)
        is_dw = s == extra
        c = jnp.where(is_dw, -9, jnp.where(s < extra, s, s - 1))
        last = s == nch
        flow = (c >= -1) & (s < nch)
        pl.when(c >= 0)(lambda: stat_wait(c))
        pl.when(flow)(lambda: phase_one(c, 0, mid, True))
        pl.when(last)(lambda: phase_one(c, 0, mid, False))
        pl.when(is_dw)(lambda: norm_back(1))
        rs_step(1, 1, s - 1)
        pl.when(s == extra + 1)(lambda: rs_step(1, 0, extra))
        pl.when((s >= 0) & (s < nq))(lambda: ag_tick(2 * s + 6))
        pl.when(flow)(lambda: phase_one(c, mid, n_tiles, True))

        @pl.when(last)
        def _():
            phase_one(c, mid, n_tiles, False)
            pl.semaphore_signal(free_sem, inc=1, device_id=partner, device_id_type=MESH)
        pl.when(is_dw)(dw_begin)
        rs_step(3, 0, s - 2)
        pl.when(s == -1)(lambda: ag_tick(5))
        pl.when(s == extra + 4)(lambda: dw_gather(2))
        pl.when(c == -1)(lambda: exp_pass(c, slot, False))
        pl.when((c >= 0) & (s < nch))(lambda: exp_pass(c, slot, True))
        pl.when(last)(lambda: dx_half(slot, 0))
        pl.when(flow)(lambda: stat_send(c + 1))
        pl.when(is_dw)(dw_join)
        rs_step(0, 0, s)
        rs_step(3, 1, s - 2)
        pl.when((c >= -2) & (c < nq - 2))(lambda: ag_finish(c + 2))

        @pl.when((c >= 0) & (c < nq - 2))
        def _():
            project(lax.rem(c + 2, nq))
            dx_half(slot, 1)
        pl.when(c >= nq - 2)(lambda: dx_half(slot, 1))
        rs_step(0, 1, s)
        pl.when((s >= 0) & (s < nq))(lambda: ag_tick(2 * s + 7))
        pl.when(s == extra + 3)(lambda: dw_gather(0))
        three(c, False)

        @pl.when(last)
        def _():
            pl.semaphore_wait(free_sem, 1)
            for h in range(2):
                give(h).start()
        rs_step(2, 0, s - 1)
        rs_step(4, 0, s - 2)
        pl.when(s == extra + 4)(lambda: dw_gather(3))
        three(c, True)
        pl.when(s != extra)(lambda: rs_step(1, 0, s))
        rs_step(2, 1, s - 1)
        rs_step(4, 1, s - 2)
        pl.when(s == -2)(lambda: ag_tick(4))
        pl.when(s == extra + 3)(lambda: dw_gather(1))
        pl.when(s == extra + 5)(lambda: dw_gather(4))

        @pl.when(s != extra)
        def _():
            x_cur[...] = x_next[...]
            x_next[...] = x_new[...]
        return carry

    lax.fori_loop(-2, nch + 1, item, 0)

    s = nch
    send_l = remote(loss_v, loss_p, misc_s.at[5], misc_r.at[5], partner)
    send_l.start()
    rs_step(1, 1, s)
    rs_step(3, 0, s - 1)
    rs_step(3, 1, s - 1)
    for h in range(2):
        give(h).wait()
    outs = []
    out_tile = rows // 8
    for j in range(8):
        r = pl.ds(pl.multiple_of(core * rows + j * out_tile, 8), out_tile)
        for h in range(2):
            lanes = slice(h * half, (h + 1) * half)
            d_e[r, lanes] = d_e[r, lanes] + zt[h * rows + j * out_tile:h * rows + (j + 1) * out_tile, :]
        outs.append(pltpu.make_async_copy(d_e.at[r], de_out.at[pl.ds(j * out_tile, out_tile)], load_sem.at[2 + j]))
        outs[-1].start()
    rs_step(2, 0, s)
    rs_step(2, 1, s)
    rs_step(4, 0, s - 1)
    rs_step(4, 1, s - 1)
    rs_step(3, 0, s)
    rs_step(3, 1, s)
    send_l.wait()
    loss_out[core] = loss_v[...]
    loss_out[1 - core] = loss_p[...]
    cnt_out[...] = counts
    norm_drain(1).wait()
    for par in range(2):
        stat_drain(par).wait_send()
    for step in range(4):
        for h in range(2):
            for d in DIRS:
                wg_copy(step, h, d).wait_send()
    remote(dw_mine, dw_other, misc_s.at[7], misc_r.at[7], partner).wait()
    for o in outs:
        o.wait()
    rs_step(4, 0, s)
    rs_step(4, 1, s)
    norm_back(0)
    save_dh = pltpu.make_async_copy(x_new.at[pl.ds(0, tok)], dh_out, load_sem.at[0])
    save_dh.start()
    norm_drain(0).wait()
    for hd in range(2):
        ln_p[0, 2 * hd:2 * hd + 2, :] = jnp.sum(ln_r[hd], axis=0)
    swap = remote(ln_p.at[0], ln_p.at[1], misc_s.at[8], misc_r.at[8], partner)
    swap.start()
    swap.wait()
    ln_out[...] = ln_p[0] + ln_p[1]
    save_dh.wait()


def solution(mesh):
    tok_spec = P(('dp', 'tp'), None)
    row_spec = P(None, ('dp', 'tp'))
    chips = mesh.shape['tp'] // CORES
    assert math.isqrt(chips) == SIDE

    def run_kernel(info, hidden, w_two, gain, bias, embed):
        tok, dim = hidden.shape
        rows = embed.shape[0]
        blk = BLOCK
        nq = tok // blk
        nch, rpc, half, quart = 2 * nq, chips * blk, dim // 2, dim // 4
        vocab = CORES * rows
        vmem = pl.BlockSpec(memory_space=pltpu.VMEM)
        hbm = pl.BlockSpec(memory_space=pltpu.MemorySpace.HBM)
        dma = pltpu.SemaphoreType.DMA
        return pl.pallas_call(
            functools.partial(fused_kernel, nq),
            out_shape=(jax.ShapeDtypeStruct((tok, dim), BF16), jax.ShapeDtypeStruct((rows, dim), F32),
                       jax.ShapeDtypeStruct((CORES, SIDE, SIDE, blk, dim), F32),
                       jax.ShapeDtypeStruct((SIDE, SIDE, blk, dim), F32), jax.ShapeDtypeStruct((4, dim), F32),
                       jax.ShapeDtypeStruct((CORES, nch, 1, rpc), F32), jax.ShapeDtypeStruct((8, 128), F32)),
            in_specs=[vmem, hbm, hbm, vmem, vmem, hbm],
            out_specs=[hbm, hbm, hbm, hbm, vmem, vmem, vmem],
            scratch_shapes=[
                pltpu.VMEM((vocab, dim), BF16), pltpu.VMEM((vocab, dim), F32),
                pltpu.VMEM((vocab, rpc), F32), pltpu.VMEM((vocab, rpc), BF16),
                pltpu.VMEM((rpc, dim), BF16), pltpu.VMEM((rpc, dim), BF16), pltpu.VMEM((rpc, dim), BF16),
                pltpu.VMEM((nq, SIDE, SIDE, blk, dim), BF16), pltpu.VMEM((dim, dim), BF16),
                pltpu.VMEM((3, SIDE, SIDE, blk, dim), F32),
                pltpu.VMEM((3, 2, 2, SIDE, blk, quart), F32), pltpu.VMEM((3, 2, 2, SIDE, blk, half), F32),
                pltpu.VMEM((3, 2, 2, blk, quart), F32), pltpu.VMEM((3, 2, 2, blk, half), F32),
                pltpu.VMEM((chips, 8, tok), F32), pltpu.VMEM((nch, 1, rpc), jnp.int32),
                pltpu.VMEM((nch, 1, rpc), F32), pltpu.VMEM((nch, 1, rpc), F32), pltpu.VMEM((2, 8, 128), F32),
                pltpu.VMEM((2, 2, rpc), F32), pltpu.VMEM((2, chips, 2, rpc), F32),
                pltpu.VMEM((8, rpc), F32), pltpu.VMEM((1, rpc), F32), pltpu.VMEM((1, rpc), F32),
                pltpu.VMEM((1, rpc), F32), pltpu.VMEM((nch, 1, rpc), F32), pltpu.VMEM((nch, 1, rpc), F32),
                pltpu.VMEM((nch, blk, dim), F32),
                pltpu.VMEM((SIDE, SIDE, blk, dim), F32), pltpu.VMEM((blk, dim), F32),
                pltpu.VMEM((2, 2, dim), F32), pltpu.VMEM((2, chips, 2, dim), F32), pltpu.VMEM((2, 4, dim), F32),
                dma((2 + nq,)), dma((nq, 4, 2, 2)), dma((nq, 4, 2, 2)), dma((3, 4, 2, 2)), dma((3, 4, 2, 2)),
                dma((2,)), dma((2,)), dma((9,)), dma((9,)), dma((2,)), dma((2,)), dma((4, 2, 2)), dma((4, 2, 2)),
                pltpu.SemaphoreType.REGULAR,
            ],
            compiler_params=pltpu.CompilerParams(collective_id=0, has_side_effects=True,
                                                 vmem_limit_bytes=VMEM_BYTES),
            name='fused_heads',
        )(info, hidden, w_two, gain, bias, embed)

    def device_step(hidden, w_two, ln_scale, ln_shift, embed, targets, loss_mask):
        tok, dim = hidden.shape
        me = lax.axis_index('tp')
        info = jnp.concatenate([targets, loss_mask, jnp.zeros((4, tok), jnp.int32)]).astype(F32)
        d_hidden, d_embed, d_w_two, _, d_norm, losses, counts = run_kernel(info, hidden, w_two, ln_scale, ln_shift, embed)
        losses = losses.reshape(CORES, 2, -1, chips, BLOCK)[:, ::-1]
        mine = lax.dynamic_index_in_dim(losses, me % CORES, 0, keepdims=False)
        token_loss = lax.dynamic_index_in_dim(mine, me // CORES, 2, keepdims=False).reshape(2, tok)
        total_loss = jnp.sum(jnp.sum(losses, axis=(0, 2, 3, 4)) / counts[2:4, 0]).reshape(1)
        return token_loss, total_loss, d_hidden, d_embed, d_w_two.reshape(dim, dim), d_norm[0::2], d_norm[1::2]

    return jax.shard_map(device_step, mesh=mesh,
                         in_specs=(tok_spec, P(), P(), P(), P('tp', None), row_spec, row_spec),
                         out_specs=(row_spec, P('dp'), tok_spec, tok_spec, P('dp', None), P('dp', None), P('dp', None)),
                         check_vma=False)
```

time: 477 us -> 361 us (0.76)
  waiting for transfers between devices: 49.5 us -> 0 us
  blocking collectives: 46.9 us -> 0 us
  between operations: 14.6 us -> 0.71 us
  matrix products: 8.39 us -> 0 us
  Pallas kernels: 336 us -> 341 us
    psum x1 -> x0, waiting for transfers between devices: 49.4 us -> none  [device_step(): lax.psum((d_w_part, d_scale_part, d_shift_part), 'tp')]
    psum x1 -> x0, blocking collectives: 46.9 us -> none  [device_step(): lax.psum((d_w_part, d_scale_part, d_shift_part), 'tp')]
    dot_general x3 -> x0, matrix products: 8.39 us -> none  [the longest x1 3.14 us: device_step(): jnp.einsum('td,ed->te', d_proj, w_two, preferred_element_type=F32)]
    pallas_call x1, Pallas kernels: 336 us -> 341 us  [run_kernel(): pl.pallas_call(functools.partial(fused_kernel, nq), out_shape=(jax.ShapeD...]
    unnamed x20 -> x5, local copies, waits for them, and re-layouts: 13.8 us -> 11.1 us
  transfers between devices with their start and end apart: 1 -> 0, of which waited for: 1 -> 0; matrix products, arithmetic and copies ran while one was open for 1% -> 0% of each run, Pallas kernels for 0% -> 0%
where the time goes in v2:
time: 361 us
  Pallas kernels  341 us (94%)
  local copies, waits for them, and re-layouts  15.4 us (4%)
    pallas_call x1, Pallas kernels, run_kernel(): pl.pallas_call(functools.partial(fused_kernel, nq), out_shape=(jax.ShapeD...  341 us
    unnamed x5, local copies, waits for them, and re-layouts  11.1 us

profile of v2, /device:TPU:97, one launch (start us, length us, event | category | flops | bytes accessed | tf_op | source)
XLA Modules:
  0.0 360.6 jit_solution(15379907488478014965)
XLA Ops:
  0.7 0.1 pad.2.clone
  0.7 1.4 add_convert_fusion.info_ref
  2.1 341.4 %fused_heads.1 = (bf16[256,1024]{1,0:T(8,128)(2,1)}, f32[1664,1024]{1,0:T(8,128)}, f32[2,4,4,32,1024]{4,3,2,1,0:T(8,128)}, f32[4,4,32,1024]{3,2,1,0:T(8,128)}, f...) custom-call(f32[8,256]{1,0:T(8,128)} %add_convert_fusion.info_ref, bf16[256,1024]{1,0:T(8,128)(2,1)} %hid_ref.1, ...), custom_call_target="tpu_custom_call" | custom-call | tf_op jit(solution)/shard_map/fused_heads/pallas_call | solution.py:589
  343.5 1.0 reduce
  344.5 0.8 slice_reduce_fusion
  345.3 1.3 slice.11
  346.6 1.3 slice.10
  347.9 0.1 reshape.29
  348.1 0.1 reverse_reduce_fusion
  348.2 0.6 divide_reduce_fusion
  348.9 0.7 reshape.30
  349.5 1.9 copy.17
  351.4 0.0 copy-start
  351.4 7.2 %copy.18 = f32[1664,1024]{1,0:T(8,128)} copy(f32[1664,1024]{1,0:T(8,128)} %get-tuple-element.29) | data formatting | bytes 13631488
  358.6 0.0 copy-done
  358.6 2.0 copy.19
  (3 shorter events, 0.1 us)
Async XLA Ops:
  351.4 7.2 %copy-start = (f32[2,4,4,32,1024]{4,3,2,1,0:T(8,128)S(1)}, f32[2,4,4,32,1024]{4,3,2,1,0:T(8,128)}, u32[]{:S(2)}) copy-start(f32[2,4,4,32,1024]{4,3,2,1,0:T(8,128)} %get-tuple-element.17) | copy-start | bytes 12582916

commit v3 on v2

v3 whole, which is shorter than its diff:
```python
import functools
import math

import jax
import jax.numpy as jnp
from jax import lax
from jax.experimental import pallas as pl
from jax.experimental.pallas import tpu as pltpu
from jax.sharding import PartitionSpec as P

LN_EPS = 1e-5
BIG = 1e30
CORES = 2
SIDE = 4
BLOCK = 32
VMEM_BYTES = 67043328
F32 = jnp.float32
BF16 = jnp.bfloat16
MESH = pl.DeviceIdType.MESH
DIRS = (1, -1)


def guarded(cond, fn):
    if isinstance(cond, bool):
        if cond:
            fn()
    else:
        pl.when(cond)(fn)


def both(a, b):
    return a and b if isinstance(a, bool) else a & b


def layer_norm(values, gain, bias):
    mean_val = jnp.mean(values, axis=-1, keepdims=True)
    centered = values - mean_val
    variance = jnp.mean(centered * centered, axis=-1, keepdims=True)
    return centered * lax.rsqrt(variance + LN_EPS) * gain + bias


def dot(a, b, ca, cb):
    return lax.dot_general(a, b, (((ca,), (cb,)), ((), ())), preferred_element_type=F32)


def fused_kernel(nq, info_ref, hid_ref, w2_ref, gain_ref, bias_ref, emb_ref,
                 dh_out, de_out, dw_out, hop, dgain_out, dbias_out, loss_out, total_out,
                 e_all, d_e, zt, dzt, x_new, x_next, x_cur, h_all, w2, d_x, dw_part, r1, r2, r3, r4,
                 info_all, tgt_v, wgt_v, msk_v, cnt, stat_s, stat_r, m_v, lse_l, lse_v, shift_v, tgt_l, loss_v, loss_p,
                 dx_own, dw_own, ln_s, ln_r, ln_p,
                 load_sem, ag_s, ag_r, rs_s, rs_r, st_s, st_r, misc_s, misc_r, lx_s, lx_r, wg_s, wg_r, free_sem):
    nch = 2 * nq
    rows = emb_ref.shape[0]
    vocab = e_all.shape[0]
    dim = e_all.shape[1]
    half = dim // 2
    quart = dim // 4
    chips, blk = SIDE * SIDE, h_all.shape[3]
    tok = nq * blk
    turn = nq + 2
    rpc = chips * blk
    me = lax.axis_index('tp')
    core = lax.rem(me, CORES)
    chip = lax.div(me, CORES)
    yy = lax.div(chip, SIDE)
    xx = lax.rem(chip, SIDE)

    def wrap(v):
        return lax.rem(v + 2 * SIDE, SIDE)

    def dev(y, x, c):
        return {'tp': (y * SIDE + x) * CORES + c}

    partner = dev(yy, xx, 1 - core)
    peers = [dev(wrap(yy + dy), wrap(xx + dx), core) for dy in range(SIDE) for dx in range(SIDE) if dy or dx]

    def neighbour(axis, d):
        return dev(yy, wrap(xx + d), core) if axis == 0 else dev(wrap(yy + d), xx, core)

    def remote(src, dst, ssem, rsem, target):
        return pltpu.make_async_remote_copy(src_ref=src, dst_ref=dst, send_sem=ssem, recv_sem=rsem,
                                            device_id=target, device_id_type=MESH)

    my_rows = pl.ds(pl.multiple_of(core * rows, 128), rows)
    other_rows = pl.ds(pl.multiple_of((1 - core) * rows, 128), rows)
    load_e = pltpu.make_async_copy(emb_ref, e_all.at[my_rows], load_sem.at[0])
    load_w = pltpu.make_async_copy(w2_ref, w2, load_sem.at[1])
    load_h = [pltpu.make_async_copy(hid_ref.at[pl.ds(q * blk, blk)], h_all.at[q, yy, xx], load_sem.at[2 + q])
              for q in range(nq)]
    for c in load_h:
        c.start()
    load_e.start()
    load_w.start()

    barrier = pltpu.get_barrier_semaphore()
    for t in peers + [partner]:
        pl.semaphore_signal(barrier, inc=1, device_id=t, device_id_type=MESH)
    pl.semaphore_wait(barrier, len(peers) + 1)

    def coords(h):
        return (xx, yy) if h == 0 else (yy, xx)

    def sub(h, d):
        return pl.ds(h * half + (0 if d == 1 else quart), quart)

    def cols_of(h):
        return pl.ds(h * half, half)

    def gathered(buf, step, h, d, back):
        a, b = coords(h)
        if step == 0:
            pos, cols = (wrap(a - back * d), b), cols_of(h)
        elif step == 1:
            pos, cols = (wrap(a - (1 + back) * d), b), sub(h, d)
        elif step == 2:
            pos, cols = (None, wrap(b - back * d)), cols_of(h)
        else:
            pos, cols = (None, wrap(b - (1 + back) * d)), sub(h, d)
        px, py = pos if h == 0 else pos[::-1]
        py = slice(None) if py is None else py
        px = slice(None) if px is None else px
        return buf.at[py, px, :, cols]

    def ag_copy(step, h, q, d, back=0):
        k = 0 if d == 1 else 1
        r = gathered(h_all.at[q], step, h, d, back)
        return remote(r, r, ag_s.at[q, step, h, k], ag_r.at[q, step, h, k],
                      neighbour(h if step < 2 else 1 - h, d))

    def ag_start(step, q):
        for h in range(2):
            for d in DIRS:
                ag_copy(step, h, q, d).start()

    def ag_wait_recv(step, q):
        for h in range(2):
            for d in DIRS:
                ag_copy(step, h, q, d, 1).wait_recv()

    def ag_tick(k, steps=(3, 2, 1, 0)):
        for step in steps:
            q = k - step

            def go(step=step, q=q):
                if step > 0:
                    ag_wait_recv(step - 1, q)
                ag_start(step, q)
            guarded(both(q >= 0, q < nq), go)

    def ag_finish(q):
        ag_wait_recv(3, q)
        for step in range(4):
            for h in range(2):
                for d in DIRS:
                    ag_copy(step, h, q, d).wait_send()

    for c in load_h:
        c.wait()
    ag_tick(0)

    info_copies = [remote(info_ref, info_all.at[chip], misc_s.at[0], misc_r.at[0], t) for t in peers]
    for c in info_copies:
        c.start()
    info_all[chip] = info_ref[...]
    ag_tick(1)
    load_e.wait()
    send_e = remote(e_all.at[my_rows], e_all.at[my_rows], misc_s.at[1], misc_r.at[1], partner)
    send_e.start()
    ag_tick(2)
    every_info = info_all.at[pl.ds(0, chips - 1)]
    remote(every_info, every_info, misc_s.at[0], misc_r.at[0], partner).wait_recv()
    remote(every_info, every_info, misc_s.at[0], misc_r.at[0], partner).wait_send()
    total = jnp.zeros((8, rpc), F32)
    for q in range(nq):
        got = jnp.concatenate([info_all[o][:, q * blk:(q + 1) * blk] for o in range(chips)], axis=1)
        total = total + got
        for hd in range(2):
            c = (1 - hd) * nq + q
            tgt_v[c] = got[hd:hd + 1].astype(jnp.int32) - chip * vocab
            msk_v[c] = got[2 + hd:3 + hd]
    cnt[0] = jnp.broadcast_to(jnp.sum(total, axis=1, keepdims=True), cnt.shape[1:])
    send_c = remote(cnt.at[0], cnt.at[1], misc_s.at[2], misc_r.at[2], partner)
    send_c.start()
    ag_tick(3)
    send_c.wait()
    counts = cnt[0] + cnt[1]
    for hd in range(2):
        for q in range(nq):
            c = (1 - hd) * nq + q
            wgt_v[c] = msk_v[c] / counts[2 + hd:3 + hd, 0:1]
    load_w.wait()

    def part(buf, h, pos1, pos2, cols):
        px, py = (pos1, pos2) if h == 0 else (pos2, pos1)
        py = slice(None) if py is None else py
        px = slice(None) if px is None else px
        return buf.at[py, px, :, cols]

    def rs_run(step, h, buf, rslot, sslot, keep):
        a, b = coords(h)

        def copy(st, k):
            d = DIRS[k]
            if st == 0:
                src, dst = part(buf, h, wrap(a + 2), None, sub(h, d)), r1
            elif st == 1:
                src, dst = part(buf, h, wrap(a + d), None, cols_of(h)), r2
            elif st == 2:
                src, dst = part(buf, h, a, wrap(b + 2), sub(h, d)), r3
            else:
                src, dst = part(buf, h, a, wrap(b + d), cols_of(h)), r4
            return remote(src, dst.at[rslot, h, k], rs_s.at[sslot, st, h, k], rs_r.at[rslot, st, h, k],
                          neighbour(h if st < 2 else 1 - h, d))

        if step > 0:
            for k in range(2):
                copy(step - 1, k).wait_recv()
        if step == 1:
            for k, d in enumerate(DIRS):
                r = part(buf, h, wrap(a + d), None, sub(h, d))
                r[...] = r[...] + r1[rslot, h, k]
        elif step == 2:
            r = part(buf, h, a, None, cols_of(h))
            r[...] = r[...] + r2[rslot, h, 0] + r2[rslot, h, 1]
        elif step == 3:
            for k, d in enumerate(DIRS):
                r = part(buf, h, a, wrap(b + d), sub(h, d))
                r[...] = r[...] + r3[rslot, h, k]
        elif step == 4:
            keep(part(buf, h, a, b, cols_of(h))[...] + r4[rslot, h, 0] + r4[rslot, h, 1])
        if step < 4:
            for k in range(2):
                copy(step, k).start()
        else:
            for st in range(4):
                for k in range(2):
                    copy(st, k).wait_send()

    def rs_step(step, h, c):
        rem = (lambda v, n: v % n) if isinstance(c, int) else (lambda v, n: lax.rem(v + 12, n))
        slot = rem(c, 3)

        def keep(val):
            dx_own[c, :, h * half:(h + 1) * half] = val
        guarded(both(c >= 0, c < nch), lambda: rs_run(step, h, d_x.at[slot], rem(c, 2), slot, keep))

    def rs_dw(step):
        for h in range(2):
            def keep(val, h=h):
                dw_own[:, h * half:(h + 1) * half] = val
            rs_run(step, h, dw_part, 2, 3, keep)

    def stat_drain(par):
        drain = stat_r.at[par, pl.ds(0, chips - 1)]
        return remote(drain, drain, st_s.at[par], st_r.at[par], partner)

    def stat_send(e):
        par = lax.rem(e, 2)
        pl.when(e >= 2)(lambda: stat_drain(par).wait_send())
        stat_s[par, 0:1, :] = lse_l[...]
        stat_s[par, 1:2, :] = tgt_l[...]
        stat_r[par, chip] = stat_s[par]
        for t in peers:
            remote(stat_s.at[par], stat_r.at[par, chip], st_s.at[par], st_r.at[par], t).start()

    def stat_wait(e):
        par = e % 2 if isinstance(e, int) else lax.rem(e, 2)
        stat_drain(par).wait_recv()
        got = stat_r[par]

        def put():
            loss_v[e - 1] = (lse_v[...] - jnp.sum(got[:, 1, :], axis=0, keepdims=True)) * msk_v[e - 1]
        guarded(e >= 1, put)
        if isinstance(e, int):
            return
        lse = got[:, 0, :]
        top = jnp.max(lse, axis=0, keepdims=True)
        lse = top + jnp.log(jnp.sum(jnp.exp(lse - top), axis=0, keepdims=True))
        lse_v[...] = lse
        wgt = wgt_v[e]
        live = wgt > 0.0
        shift_v[...] = jnp.where(live, lse - jnp.log(jnp.where(live, wgt, 1.0)), BIG)

    tile = 256

    def project(q):
        h = h_all[q].reshape(rpc, dim)
        for n0 in range(0, dim, half):
            x_new[:, n0:n0 + half] = dot(h, w2[:, n0:n0 + half], 1, 0).astype(BF16)

    def fetch(c):
        q = lax.rem(c, nq)
        pl.when(c < nq)(lambda: project(q))

        @pl.when(c >= nq)
        def _():
            x_new[...] = h_all[q].reshape(rpc, dim)

    def norm_rows(hd, lo, hi):
        step = 64
        gain, bias = gain_ref[pl.ds(hd, 1), :], bias_ref[pl.ds(hd, 1), :]
        for r in range(lo, hi, step):
            x_new[r:r + step, :] = layer_norm(x_new[r:r + step, :].astype(F32), gain, bias).astype(BF16)

    def logits_tile(v0, top):
        z = dot(e_all[v0:v0 + tile, :], x_next[...], 1, 1)
        zt[v0:v0 + tile, :] = z
        return jnp.maximum(top, jnp.max(z.reshape(tile // 8, 8, rpc), axis=0))

    def strips(c):
        tgt = tgt_v[c]
        return jnp.where(lax.broadcasted_iota(jnp.int32, (8, rpc), 0) == (tgt & 7), tgt >> 3, -1)

    def grad_tile(v0, shift, where8, wgt):
        prob = jnp.exp(zt[v0:v0 + tile, :] - shift).reshape(tile // 8, 8, rpc)
        hit = lax.broadcasted_iota(jnp.int32, (tile // 8, 8, rpc), 0) == (where8 - v0 // 8)[None]
        dzt[v0:v0 + tile, :] = jnp.where(hit, prob - wgt[None], prob).reshape(tile, rpc).astype(BF16)

    n_tiles = vocab // tile

    def phase_one(c, with_logits):
        at = jnp.maximum(c, 0)
        shift, where8, wgt = shift_v[...], strips(at), wgt_v[at]
        top = jnp.full((8, rpc), -jnp.inf, F32)
        for j in range(n_tiles):
            grad_tile(j * tile, shift, where8, wgt)
            if with_logits:
                top = logits_tile(j * tile, top)
        if with_logits:
            m_v[...] = top

    def dx_half(slot, h):
        val = dot(dzt[...], e_all[:, h * half:(h + 1) * half], 0, 0)
        d_x[slot, :, :, :, h * half:(h + 1) * half] = val.reshape(SIDE, SIDE, blk, half)

    def exp_pass(slot=None):
        top = jnp.max(m_v[...], axis=0, keepdims=True)
        acc = jnp.zeros((8, rpc), F32)
        for j in range(n_tiles):
            prob = jnp.exp(zt[j * tile:(j + 1) * tile, :] - top)
            acc = acc + jnp.sum(prob.reshape(tile // 8, 8, rpc), axis=0)
        if slot is not None:
            dx_half(slot, 0)
        lse_l[...] = top + jnp.log(jnp.sum(acc, axis=0, keepdims=True))

    de_tile = rows // 4

    def phase_three(c, with_grad, norm):
        hd = jnp.where(c + 2 < nq, 1, 0)
        where8 = strips(jnp.clip(c + 1, 0, nch - 1))
        found = jnp.zeros((8, rpc), F32)
        if with_grad and norm:
            dx_half(lax.rem(c + 3, 3), 1)
        for j in range(8):
            base = (core if j >= 4 else 1 - core) * rows
            if norm:
                norm_rows(hd, j * rpc // 8, (j + 1) * rpc // 8)
                for v0 in range(j * de_tile, (j + 1) * de_tile, 8):
                    found = jnp.where(where8 == v0 // 8, zt[v0:v0 + 8, :], found)
            if with_grad:
                r = pl.ds(pl.multiple_of(base + j % 4 * de_tile, 32), de_tile)
                d_e[r, :] = d_e[r, :] + dot(dzt[r, :], x_cur[...], 1, 0)
        tgt_l[...] = jnp.sum(found, axis=0, keepdims=True)

    def own_hidden(j, n, lanes=slice(None)):
        return h_all[j:j + n, yy, xx, :, lanes].reshape(n * blk, -1)

    def norm_back(hd, lo=0, hi=nq // 2):
        step = 2 * blk
        d_gain = jnp.zeros((8, dim), F32)
        d_bias = jnp.zeros((8, dim), F32)
        if hd == 1:
            for n0 in range(0, dim, half):
                x_new[0:tok, n0:n0 + half] = dot(own_hidden(0, nq), w2[:, n0:n0 + half], 1, 0).astype(BF16)
        for j in range(lo, hi):
            r = j * step
            val = (x_new[r:r + step, :] if hd == 1 else own_hidden(2 * j, 2)).astype(F32)
            cen = val - jnp.mean(val, axis=-1, keepdims=True)
            rstd = lax.rsqrt(jnp.mean(cen * cen, axis=-1, keepdims=True) + LN_EPS)
            hat = cen * rstd
            at = (1 - hd) * nq + 2 * j
            d_y = dx_own[at:at + 2].reshape(step, dim)
            d_gain = d_gain + jnp.sum((d_y * hat).reshape(step // 8, 8, dim), axis=0)
            d_bias = d_bias + jnp.sum(d_y.reshape(step // 8, 8, dim), axis=0)
            g = d_y * gain_ref[hd:hd + 1, :]
            d_in = rstd * (g - jnp.mean(g, axis=-1, keepdims=True) - hat * jnp.mean(g * hat, axis=-1, keepdims=True))
            if hd == 1:
                x_new[tok + r:tok + r + step, :] = d_in.astype(BF16)
            else:
                x_new[r:r + step, :] = (d_in + dx_own[2 * j:2 * j + 2].reshape(step, dim)).astype(BF16)
        sums = (jnp.sum(d_gain, axis=0, keepdims=True), jnp.sum(d_bias, axis=0, keepdims=True))
        for k in range(2):
            ln_s[hd, k:k + 1, :] = sums[k] if lo == 0 else ln_s[hd, k:k + 1, :] + sums[k]
        if hi < nq // 2:
            return
        ln_r[hd, chip] = ln_s[hd]
        for t in peers:
            remote(ln_s.at[hd], ln_r.at[hd, chip], lx_s.at[hd], lx_r.at[hd], t).start()

    def norm_drain(hd):
        drain = ln_r.at[hd, pl.ds(0, chips - 1)]
        return remote(drain, drain, lx_s.at[hd], lx_r.at[hd], partner)

    dw_half_rows = SIDE // 2

    def dw_rows(k, p):
        lanes = pl.ds(pl.multiple_of(k * half + p * quart, quart), quart)
        return dot(own_hidden(0, nq, lanes), x_new[tok:2 * tok, :], 0, 0)

    def send_hop(p):
        stage = dx_own.at[pl.ds((1 - p) * nq, nq)]
        return remote(stage, hop.at[p], misc_s.at[6 + p], misc_r.at[6 + p], partner)

    def load_hop(p):
        return pltpu.make_async_copy(hop.at[p], dx_own.at[pl.ds(nq, nq)], load_sem.at[0])

    def dw_begin():
        norm_back(1)
        for p in range(2):
            dx_own[(1 - p) * nq:(2 - p) * nq] = dw_rows(1 - core, p).reshape(nq, blk, dim)
            send_hop(p).start()
        for p in range(2):
            dw_part[p * dw_half_rows:(p + 1) * dw_half_rows] = dw_rows(core, p).reshape(dw_half_rows, SIDE, blk, dim)

    def dw_mid():
        for p in range(2):
            send_hop(p).wait()
        load_hop(0).start()
        dx_own[0:nq] = dot(x_new[tok:2 * tok, :], w2[...], 1, 1).reshape(nq, blk, dim)

    def dw_add(p):
        load_hop(p).wait()
        r = dw_part.at[pl.ds(p * dw_half_rows, dw_half_rows)]
        r[...] = r[...] + dx_own[nq:2 * nq].reshape(dw_half_rows, SIDE, blk, dim)
        if p == 0:
            load_hop(1).start()
        else:
            rs_dw(0)

    dw_mine = dw_out.at[core]
    save_dw = pltpu.make_async_copy(dw_own, dw_out.at[core, yy, xx], load_sem.at[1])
    send_dw = remote(dw_mine, dw_mine, misc_s.at[9], misc_r.at[9], partner)
    dw_other = dw_out.at[1 - core]

    def wg_copy(step, h, d, back=0):
        k = 0 if d == 1 else 1
        r = gathered(dw_mine, step, h, d, back)
        src = dw_own.at[:, cols_of(h)] if step == 0 and not back else r
        return remote(src, r, wg_s.at[step, h, k], wg_r.at[step, h, k], neighbour(h if step < 2 else 1 - h, d))

    def dw_gather(step):
        if step == 0:
            save_dw.start()
        else:
            for h in range(2):
                for d in DIRS:
                    wg_copy(step - 1, h, d, 1).wait_recv()
        if step == 2:
            save_dw.wait()
        if step == 4:
            send_dw.start()
            return
        for h in range(2):
            for d in DIRS:
                wg_copy(step, h, d).start()

    def give(h):
        lanes = slice(h * half, (h + 1) * half)
        return remote(d_e.at[other_rows, lanes], zt.at[pl.ds(h * rows, rows)], misc_s.at[3 + h], misc_r.at[3 + h], partner)

    m_v[...] = jnp.zeros(m_v.shape, F32)
    lse_v[...] = jnp.zeros(lse_v.shape, F32)
    lse_l[...] = jnp.zeros(lse_l.shape, F32)
    shift_v[...] = jnp.zeros(shift_v.shape, F32)
    remote(e_all.at[other_rows], e_all.at[other_rows], misc_s.at[1], misc_r.at[1], partner).wait()

    def chunk(i, carry):
        c = i - 2
        slot = lax.rem(i + 1, 3)
        last = c == nch - 1
        flow = (c >= -1) & (c < nch - 1)

        def at(k, fn):
            pl.when(c == k)(fn)

        pl.when(c >= 0)(lambda: stat_wait(c))
        pl.when(flow)(lambda: phase_one(c, True))
        rs_step(4, 1, c - 3)

        @pl.when(last)
        def _():
            phase_one(c, False)
            dx_half(slot, 0)
            dx_half(slot, 1)
        rs_step(2, 1, c - 2)
        rs_step(3, 0, c - 2)
        rs_step(1, 0, c - 1)
        at(turn, dw_begin)
        at(turn + 3, lambda: rs_dw(3))
        at(0, lambda: ag_tick(6))
        at(-1, exp_pass)

        @pl.when((c >= 0) & (c < nch - 1))
        def _():
            exp_pass(slot)
        pl.when(c >= -1)(lambda: stat_send(c + 1))
        rs_step(0, 0, c)
        pl.when(last)(lambda: rs_step(0, 1, c))
        rs_step(1, 1, c - 1)
        at(turn, dw_mid)
        at(turn + 1, lambda: rs_dw(1))
        at(turn + 4, lambda: dw_gather(1))
        at(-1, lambda: ag_tick(5))
        pl.when(c < nq - 2)(lambda: ag_finish(c + 2))
        pl.when(c < nch - 2)(lambda: fetch(c + 2))
        pl.when(c < 0)(lambda: phase_three(c, False, True))
        pl.when((c >= 0) & (c < nch - 1))(lambda: phase_three(c, True, True))
        pl.when(last)(lambda: phase_three(c, True, False))

        @pl.when(c == -1)
        def _():
            d_e[...] = jnp.zeros(d_e.shape, F32)

        @pl.when(last)
        def _():
            rs_step(1, 0, c)
            rs_step(1, 1, c)
        rs_step(2, 0, c - 1)
        pl.when(c < nch - 1)(lambda: rs_step(0, 1, c))

        @pl.when(c == turn)
        def _():
            dw_add(0)
            dw_add(1)
        rs_step(3, 1, c - 2)
        rs_step(4, 0, c - 2)
        at(turn + 2, lambda: rs_dw(2))

        @pl.when(c == turn + 3)
        def _():
            rs_dw(4)
            dw_gather(0)
        at(turn + 4, lambda: dw_gather(2))
        pl.when((c >= 1) & (c <= 3))(lambda: ag_tick(c + 7, (3, 2, 1)))
        at(-2, lambda: ag_tick(4))
        at(0, lambda: ag_tick(7))
        x_cur[...] = x_next[...]
        x_next[...] = x_new[...]
        return carry

    lax.fori_loop(0, nch + 2, chunk, 0)

    c = nch - 1
    pl.semaphore_signal(free_sem, inc=1, device_id=partner, device_id_type=MESH)
    dw_gather(3)
    stat_wait(nch)
    send_l = remote(loss_v, loss_p, misc_s.at[5], misc_r.at[5], partner)
    send_l.start()
    pl.semaphore_wait(free_sem, 1)
    for h in range(2):
        give(h).start()
    rs_step(4, 1, c - 2)
    rs_step(2, 1, c - 1)
    rs_step(3, 0, c - 1)
    rs_step(2, 0, c)
    rs_step(2, 1, c)
    rs_step(3, 1, c - 1)
    rs_step(4, 0, c - 1)
    rs_step(3, 0, c)
    rs_step(3, 1, c)
    rs_step(4, 1, c - 1)
    dw_gather(4)
    for h in range(2):
        give(h).wait()
    outs = []
    out_tile = rows // 8
    for j in range(8):
        r = pl.ds(pl.multiple_of(core * rows + j * out_tile, 8), out_tile)
        for h in range(2):
            lanes = slice(h * half, (h + 1) * half)
            d_e[r, lanes] = d_e[r, lanes] + zt[h * rows + j * out_tile:h * rows + (j + 1) * out_tile, :]
        outs.append(pltpu.make_async_copy(d_e.at[r], de_out.at[pl.ds(j * out_tile, out_tile)], load_sem.at[2 + j]))
        outs[-1].start()
    send_l.wait()
    mine = jnp.concatenate([loss_v[k] for k in range(nch)], axis=0)
    every = jnp.sum(mine + jnp.concatenate([loss_p[k] for k in range(nch)], axis=0), axis=1, keepdims=True)
    total_out[...] = sum(jnp.sum(every[(1 - hd) * nq:(2 - hd) * nq], axis=0, keepdims=True) / counts[2 + hd:3 + hd, 0:1]
                         for hd in range(2))
    own = mine[:, 0:blk]
    for o in range(1, chips):
        own = jnp.where(chip == o, mine[:, o * blk:(o + 1) * blk], own)
    for hd in range(2):
        k = (1 - hd) * nq
        loss_out[hd:hd + 1, :] = jnp.concatenate([own[k + q:k + q + 1] for q in range(nq)], axis=1)
    norm_drain(1).wait()
    for par in range(2):
        stat_drain(par).wait_send()
    for step in range(4):
        for h in range(2):
            for d in DIRS:
                wg_copy(step, h, d).wait_send()
    remote(dw_mine, dw_other, misc_s.at[9], misc_r.at[9], partner).wait()
    for o in outs:
        o.wait()
    norm_back(0, 0, nq // 2 - 1)
    rs_step(4, 0, c)
    rs_step(4, 1, c)
    norm_back(0, nq // 2 - 1)
    save_dh = pltpu.make_async_copy(x_new.at[pl.ds(0, tok)], dh_out, load_sem.at[0])
    save_dh.start()
    norm_drain(0).wait()
    for hd in range(2):
        ln_p[0, 2 * hd:2 * hd + 2, :] = jnp.sum(ln_r[hd], axis=0)
    swap = remote(ln_p.at[0], ln_p.at[1], misc_s.at[8], misc_r.at[8], partner)
    swap.start()
    swap.wait()
    for hd in range(2):
        k = 2 * hd
        dgain_out[hd:hd + 1, :] = ln_p[0, k:k + 1, :] + ln_p[1, k:k + 1, :]
        dbias_out[hd:hd + 1, :] = ln_p[0, k + 1:k + 2, :] + ln_p[1, k + 1:k + 2, :]
    save_dh.wait()


def copy_kernel(de_in, dw_in, dh_in, a_in, b_in, c_in, d_in, de_out, dw_out, dh_out, a_out, b_out, c_out, d_out,
                de_v, dw_v, dh_v, in_sem, out_sem):
    jobs = []
    for src, buf, dst, tiles in ((de_in, de_v, de_out, 8), (dw_in, dw_v, dw_out, 4), (dh_in, dh_v, dh_out, 1)):
        n = src.shape[0] // tiles
        jobs += [(src.at[pl.ds(j * n, n)], buf.at[pl.ds(j * n, n)], dst.at[pl.ds(j * n, n)]) for j in range(tiles)]
    loads = [pltpu.make_async_copy(src, buf, in_sem.at[j]) for j, (src, buf, _) in enumerate(jobs)]
    saves = [pltpu.make_async_copy(buf, dst, out_sem.at[j]) for j, (_, buf, dst) in enumerate(jobs)]
    for c in loads:
        c.start()
    for src, dst in ((a_in, a_out), (b_in, b_out), (c_in, c_out), (d_in, d_out)):
        dst[...] = src[...]
    for load, save in zip(loads, saves):
        load.wait()
        save.start()
    for c in saves:
        c.wait()


def solution(mesh):
    tok_spec = P(('dp', 'tp'), None)
    row_spec = P(None, ('dp', 'tp'))
    chips = mesh.shape['tp'] // CORES
    assert math.isqrt(chips) == SIDE

    def run_kernel(info, hidden, w_two, gain, bias, embed):
        tok, dim = hidden.shape
        rows = embed.shape[0]
        blk = BLOCK
        nq = tok // blk
        nch, rpc, half, quart = 2 * nq, chips * blk, dim // 2, dim // 4
        vocab = CORES * rows
        vmem = pl.BlockSpec(memory_space=pltpu.VMEM)
        hbm = pl.BlockSpec(memory_space=pltpu.MemorySpace.HBM)
        dma = pltpu.SemaphoreType.DMA
        return pl.pallas_call(
            functools.partial(fused_kernel, nq),
            out_shape=(jax.ShapeDtypeStruct((tok, dim), BF16), jax.ShapeDtypeStruct((rows, dim), F32),
                       jax.ShapeDtypeStruct((CORES, SIDE, SIDE, blk, dim), F32),
                       jax.ShapeDtypeStruct((2, nq, blk, dim), F32), jax.ShapeDtypeStruct((2, dim), F32),
                       jax.ShapeDtypeStruct((2, dim), F32), jax.ShapeDtypeStruct((2, tok), F32),
                       jax.ShapeDtypeStruct((1, 1), F32)),
            in_specs=[vmem, hbm, hbm, vmem, vmem, hbm],
            out_specs=[hbm, hbm, hbm, hbm, vmem, vmem, vmem, vmem],
            scratch_shapes=[
                pltpu.VMEM((vocab, dim), BF16), pltpu.VMEM((vocab, dim), F32),
                pltpu.VMEM((vocab, rpc), F32), pltpu.VMEM((vocab, rpc), BF16),
                pltpu.VMEM((rpc, dim), BF16), pltpu.VMEM((rpc, dim), BF16), pltpu.VMEM((rpc, dim), BF16),
                pltpu.VMEM((nq, SIDE, SIDE, blk, dim), BF16), pltpu.VMEM((dim, dim), BF16),
                pltpu.VMEM((3, SIDE, SIDE, blk, dim), F32), pltpu.VMEM((SIDE, SIDE, blk, dim), F32),
                pltpu.VMEM((3, 2, 2, SIDE, blk, quart), F32), pltpu.VMEM((3, 2, 2, SIDE, blk, half), F32),
                pltpu.VMEM((3, 2, 2, blk, quart), F32), pltpu.VMEM((3, 2, 2, blk, half), F32),
                pltpu.VMEM((chips, 8, tok), F32), pltpu.VMEM((nch, 1, rpc), jnp.int32),
                pltpu.VMEM((nch, 1, rpc), F32), pltpu.VMEM((nch, 1, rpc), F32), pltpu.VMEM((2, 8, 128), F32),
                pltpu.VMEM((2, 2, rpc), F32), pltpu.VMEM((2, chips, 2, rpc), F32),
                pltpu.VMEM((8, rpc), F32), pltpu.VMEM((1, rpc), F32), pltpu.VMEM((1, rpc), F32),
                pltpu.VMEM((1, rpc), F32), pltpu.VMEM((1, rpc), F32),
                pltpu.VMEM((nch, 1, rpc), F32), pltpu.VMEM((nch, 1, rpc), F32),
                pltpu.VMEM((nch, blk, dim), F32),
                pltpu.VMEM((blk, dim), F32),
                pltpu.VMEM((2, 2, dim), F32), pltpu.VMEM((2, chips, 2, dim), F32), pltpu.VMEM((2, 4, dim), F32),
                dma((2 + nq,)), dma((nq, 4, 2, 2)), dma((nq, 4, 2, 2)), dma((4, 4, 2, 2)), dma((3, 4, 2, 2)),
                dma((2,)), dma((2,)), dma((10,)), dma((10,)), dma((2,)), dma((2,)), dma((4, 2, 2)), dma((4, 2, 2)),
                pltpu.SemaphoreType.REGULAR,
            ],
            compiler_params=pltpu.CompilerParams(collective_id=0, has_side_effects=True,
                                                 vmem_limit_bytes=VMEM_BYTES),
            name='fused_heads',
        )(info, hidden, w_two, gain, bias, embed)

    def device_step(hidden, w_two, ln_scale, ln_shift, embed, targets, loss_mask):
        tok, dim = hidden.shape
        info = jnp.concatenate([targets, loss_mask, jnp.zeros((4, tok), jnp.int32)]).astype(F32)
        d_hidden, d_embed, d_w_two, _, d_scale, d_shift, token_loss, total_loss = run_kernel(
            info, hidden, w_two, ln_scale, ln_shift, embed)
        d_w_two = d_w_two.reshape(dim, dim)
        arrays = (d_embed, d_w_two, d_hidden, d_scale, d_shift, token_loss, total_loss)
        specs = [pl.BlockSpec(memory_space=pltpu.MemorySpace.HBM)] * 3 + [pl.BlockSpec(memory_space=pltpu.VMEM)] * 4
        d_embed, d_w_two, d_hidden, d_scale, d_shift, token_loss, total_loss = pl.pallas_call(
            copy_kernel, out_shape=tuple(jax.ShapeDtypeStruct(v.shape, v.dtype) for v in arrays),
            in_specs=specs, out_specs=specs,
            scratch_shapes=[pltpu.VMEM(v.shape, v.dtype) for v in arrays[:3]] + [pltpu.SemaphoreType.DMA((13,))] * 2,
            compiler_params=pltpu.CompilerParams(vmem_limit_bytes=VMEM_BYTES), name='store_results',
        )(*arrays)
        return (token_loss, total_loss.reshape(1), d_hidden, d_embed, d_w_two, d_scale, d_shift)

    return jax.shard_map(device_step, mesh=mesh,
                         in_specs=(tok_spec, P(), P(), P(), P('tp', None), row_spec, row_spec),
                         out_specs=(row_spec, P('dp'), tok_spec, tok_spec, P('dp', None), P('dp', None), P('dp', None)),
                         check_vma=False)
```

time: 361 us -> 332 us (0.920)
  local copies, waits for them, and re-layouts: 15.4 us -> 0.08 us
  Pallas kernels: 341 us -> 329 us
    pallas_call x1, Pallas kernels: 341 us -> 318 us  [run_kernel(): pl.pallas_call(functools.partial(fused_kernel, nq), out_shape=(jax.ShapeD...]
    unnamed x5 -> x0, local copies, waits for them, and re-layouts: 11.1 us -> none
    pallas_call x0 -> x1, Pallas kernels: none -> 10.6 us  [device_step(): pl.pallas_call(copy_kernel, out_shape=tuple((jax.ShapeDtypeStruct(v.shape...]
where the time goes in v3:
time: 332 us; the launch traced here: 331 us
  Pallas kernels  329 us (99%)
    pallas_call x1, Pallas kernels, run_kernel(): pl.pallas_call(functools.partial(fused_kernel, nq), out_shape=(jax.ShapeD...  318 us
    pallas_call x1, Pallas kernels, device_step(): pl.pallas_call(copy_kernel, out_shape=tuple((jax.ShapeDtypeStruct(v.shape...  10.6 us

profile of v3, /device:TPU:97, one launch (start us, length us, event | category | flops | bytes accessed | tf_op | source)
XLA Modules:
  0.0 331.3 jit_solution(11163944177810974755)
XLA Ops:
  0.6 0.1 pad.2.clone
  0.7 1.4 add_convert_fusion.info_ref
  2.1 318.5 %fused_heads.1 = (bf16[256,1024]{1,0:T(8,128)(2,1)}, f32[1664,1024]{1,0:T(8,128)}, f32[2,4,4,32,1024]{4,3,2,1,0:T(8,128)}, f32[2,8,32,1024]{3,2,1,0:T(8,128)}, f...) custom-call(f32[8,256]{1,0:T(8,128)} %add_convert_fusion.info_ref, ...), custom_call_target="tpu_custom_call" | custom-call | tf_op jit(solution)/shard_map/fused_heads/pallas_call | solution.py:659
  320.6 10.6 %store_results.1 = (f32[1664,1024]{1,0:T(8,128)}, f32[1024,1024]{1,0:T(8,128)}, bf16[256,1024]{1,0:T(8,128)(2,1)}, f32[2,1024]{1,0:T(2,128)}, f32[2,1024]{1,0:T(...) custom-call(f32[1664,1024]{1,0:T(8,128)} %get-tuple-element.21.de_in, f32[1024,1024]{1,0:T(8,128)} %bitcast.2, ...), custom_call_target="tpu_custom_call" | custom-call | tf_op jit(solution)/shard_map/store_results/pallas_call | solution.py:702
  (1 shorter events, 0.0 us)
